TPU v7x, 8 devices: a whole 2x2x1 slice. The times are simulated.
8 devices in a mesh: dp: 4 (over z, y, x), tp: 2 (over core).
Axes of the slice: x: 2, y: 2, z: 1, core: 2. Of those that a mesh axis runs over, the one named last changes fastest.
Arguments:
- x_teach: bfloat16 [16, 256, 1024], P('dp', 'tp')
- x_stud: bfloat16 [16, 256, 768], P(('dp', 'tp'))
- w_up_t: bfloat16 [8, 1024, 4096], P(None, None, 'tp')
- w_down_t: bfloat16 [8, 4096, 1024], P(None, 'tp')
- gain_t: float32 [8, 1024], replicated
- head_t: bfloat16 [1024, 50304], P(None, 'tp')
- w_up_s: bfloat16 [1, 768, 3072], replicated
- w_down_s: bfloat16 [1, 3072, 768], replicated
- gain_s: float32 [1, 768], replicated
- proj_s: bfloat16 [1, 768, 1024], replicated
- head_s: bfloat16 [768, 50304], replicated
Outputs:
- output 1: float32 [], replicated
- output 2: float32 [1, 768, 3072], replicated
- output 3: float32 [1, 3072, 768], replicated
- output 4: float32 [1, 768], replicated
- output 5: float32 [1, 768, 1024], replicated
- output 6: float32 [768, 50304], replicated
All inputs are finite; a program needn't handle non-finite values.
Results may differ from a plain program's by a relative error of at most 0.0168161.
Values are sent between devices in bfloat16 or wider.
A program may use at most 1.5 GiB of HBM per device.

v0:
```python
import jax
import jax.numpy as jnp
from jax import lax
from jax.sharding import PartitionSpec as P

NORM_EPS = 1e-6


def rms_parts(values):
    vals32 = values.astype(jnp.float32)
    inv_rms = lax.rsqrt(jnp.mean(vals32 * vals32, axis=-1, keepdims=True) + NORM_EPS)
    return vals32 * inv_rms, inv_rms


def rms_back(normed, inv_rms, grad_out):
    return inv_rms * (grad_out - normed * jnp.mean(grad_out * normed, axis=-1, keepdims=True))


def gelu_tanh(values):
    return jax.nn.gelu(values, approximate=True)


def gelu_back(pre_act, grad_out):
    return jax.vjp(gelu_tanh, pre_act)[1](grad_out)[0]


def mat_mul(subscripts, lhs_arr, rhs_arr):
    return jnp.einsum(subscripts, lhs_arr, rhs_arr, preferred_element_type=jnp.float32)


def student_forward(x_stud, w_up_s, w_down_s, gain_s, proj_s, features):
    residual = x_stud.astype(jnp.float32)
    norm_cur, inv_cur = rms_parts(residual)
    saved_acts = []
    err_total = jnp.zeros((), jnp.float32)
    for layer_idx in range(w_up_s.shape[0]):
        normed = (norm_cur * gain_s[layer_idx]).astype(jnp.bfloat16)
        pre_act = mat_mul('bsd,df->bsf', normed, w_up_s[layer_idx])
        hidden_act = gelu_tanh(pre_act).astype(jnp.bfloat16)
        residual = residual + mat_mul('bsf,fd->bsd', hidden_act, w_down_s[layer_idx])
        norm_next, inv_next = rms_parts(residual)
        proj_in = norm_next.astype(jnp.bfloat16)
        feat_err = mat_mul('bsd,de->bse', proj_in, proj_s[layer_idx]) - features[layer_idx]
        err_total = err_total + jnp.sum(feat_err * feat_err)
        saved_acts.append((norm_cur, inv_cur, normed, pre_act, hidden_act, norm_next, inv_next, proj_in, feat_err))
        norm_cur, inv_cur = norm_next, inv_next
    return saved_acts, err_total


def student_backward(saved_acts, w_up_s, w_down_s, gain_s, proj_s, feat_coef, head_in_grad):
    n_layers = len(saved_acts)
    up_grads = []
    down_grads = []
    gain_grads = []
    proj_grads = []
    resid_grad = None
    for layer_idx in reversed(range(n_layers)):
        norm_cur, inv_cur, normed, pre_act, hidden_act, norm_next, inv_next, proj_in, feat_err = saved_acts[layer_idx]
        err_grad = (2.0 * feat_coef * feat_err).astype(jnp.bfloat16)
        proj_grads.append(mat_mul('bsd,bse->de', proj_in, err_grad))
        out_grad = mat_mul('bse,de->bsd', err_grad, proj_s[layer_idx])
        if resid_grad is None:
            resid_grad = rms_back(norm_next, inv_next, out_grad + head_in_grad)
        else:
            resid_grad = resid_grad + rms_back(norm_next, inv_next, out_grad)
        resid_bf = resid_grad.astype(jnp.bfloat16)
        down_grads.append(mat_mul('bsf,bsd->fd', hidden_act, resid_bf))
        act_grad = mat_mul('bsd,fd->bsf', resid_bf, w_down_s[layer_idx])
        pre_grad = gelu_back(pre_act, act_grad).astype(jnp.bfloat16)
        up_grads.append(mat_mul('bsd,bsf->df', normed, pre_grad))
        norm_grad = mat_mul('bsf,df->bsd', pre_grad, w_up_s[layer_idx])
        gain_grads.append(jnp.sum(norm_grad * norm_cur, axis=(0, 1)))
        if layer_idx > 0:
            resid_grad = resid_grad + rms_back(norm_cur, inv_cur, norm_grad * gain_s[layer_idx])
    return (jnp.stack(up_grads[::-1]), jnp.stack(down_grads[::-1]),
            jnp.stack(gain_grads[::-1]), jnp.stack(proj_grads[::-1]))


def solution(mesh):
    dp_size = mesh.shape['dp']
    tp_size = mesh.shape['tp']

    def local_step(x_teach, x_stud, w_up_t, w_down_t, gain_t, head_t, w_up_s, w_down_s, gain_s, proj_s, head_s):
        n_feat = w_up_s.shape[0]
        per_feat = w_up_t.shape[0] // n_feat
        hidden = x_teach
        features = []
        for layer_idx in range(w_up_t.shape[0]):
            normed = (rms_parts(hidden)[0] * gain_t[layer_idx]).astype(jnp.bfloat16)
            gathered = lax.all_gather(normed, 'tp', axis=1, tiled=True)
            hidden_act = gelu_tanh(mat_mul('bsd,df->bsf', gathered, w_up_t[layer_idx])).astype(jnp.bfloat16)
            partial_out = mat_mul('bsf,fd->bsd', hidden_act, w_down_t[layer_idx])
            layer_out = lax.psum_scatter(partial_out, 'tp', scatter_dimension=1, tiled=True)
            hidden = hidden + layer_out.astype(jnp.bfloat16)
            if (layer_idx + 1) % per_feat == 0:
                features.append(lax.all_to_all(hidden, 'tp', 0, 1, tiled=True))
        final_norm = rms_parts(hidden)[0].astype(jnp.bfloat16)
        final_full = lax.all_gather(final_norm, 'tp', axis=1, tiled=True)
        teach_logits = mat_mul('bsd,dv->bsv', final_full, head_t)

        n_tokens = x_stud.shape[0] * x_stud.shape[1] * dp_size * tp_size
        feat_coef = 1.0 / (n_feat * n_tokens * head_t.shape[0])
        kl_coef = 1.0 / n_tokens
        saved_acts, err_total = student_forward(x_stud, w_up_s, w_down_s, gain_s, proj_s, features)
        head_in = saved_acts[-1][7]
        stud_full = lax.all_gather(head_in, 'tp', axis=0, tiled=True)
        vocab_part = head_t.shape[1]
        head_cols = lax.dynamic_slice_in_dim(head_s, lax.axis_index('tp') * vocab_part, vocab_part, axis=1)
        stud_logits = mat_mul('bsd,dv->bsv', stud_full, head_cols)
        peak_vals = lax.pmax(jnp.stack([jnp.max(teach_logits, axis=-1), jnp.max(stud_logits, axis=-1)]), 'tp')
        teach_exp = jnp.exp(teach_logits - peak_vals[0][..., None])
        stud_exp = jnp.exp(stud_logits - peak_vals[1][..., None])
        sum_vals = lax.psum(jnp.stack([jnp.sum(teach_exp, axis=-1), jnp.sum(stud_exp, axis=-1)]), 'tp')
        log_norms = peak_vals + jnp.log(sum_vals)
        teach_prob = teach_exp / sum_vals[0][..., None]
        stud_prob = stud_exp / sum_vals[1][..., None]
        log_ratio = teach_logits - stud_logits - (log_norms[0] - log_norms[1])[..., None]
        kl_local = jnp.sum(teach_prob * log_ratio)
        logit_grad = (kl_coef * (stud_prob - teach_prob)).astype(jnp.bfloat16)
        head_part = mat_mul('bsd,bsv->dv', stud_full, logit_grad)
        head_grad = lax.all_gather(lax.psum(head_part, 'dp'), 'tp', axis=1, tiled=True)
        full_in_grad = mat_mul('bsv,dv->bsd', logit_grad, head_cols)
        head_in_grad = lax.psum_scatter(full_in_grad, 'tp', scatter_dimension=0, tiled=True)
        local_grads = student_backward(saved_acts, w_up_s, w_down_s, gain_s, proj_s, feat_coef, head_in_grad)
        grad_up, grad_down, grad_gain, grad_proj = lax.psum(local_grads, ('dp', 'tp'))
        total_loss = lax.psum(feat_coef * err_total + kl_coef * kl_local, ('dp', 'tp'))
        return total_loss, grad_up, grad_down, grad_gain, grad_proj, head_grad

    in_specs = (P('dp', 'tp', None), P(('dp', 'tp'), None, None), P(None, None, 'tp'), P(None, 'tp', None),
                P(), P(None, 'tp'), P(), P(), P(), P(), P())
    out_specs = (P(), P(), P(), P(), P(), P())
    return jax.shard_map(local_step, mesh=mesh, in_specs=in_specs, out_specs=out_specs, check_vma=False)
```

profile of v0, /device:TPU:0, one launch (start us, length us, event | category | flops | bytes accessed | tf_op | source)
XLA Modules:
  0.0 2447.5 jit_solution(5344350413821691165)
XLA Ops:
  13.1 10.7 all-gather.12.cloned.1.call-done
  23.8 6.9 fusion.120
  30.7 9.3 fusion.118
  40.1 10.5 reduce-scatter.10.cloned.1.call-done
  55.0 9.1 all-gather.14.cloned.1.call-done
  64.1 15.0 fusion.114
  79.2 10.5 reduce-scatter.12.cloned.1.call-done
  93.6 9.0 all-gather.16.cloned.1.call-done
  102.6 15.0 fusion.110
  117.7 10.5 reduce-scatter.14.cloned.1.call-done
  132.7 9.0 all-gather.18.cloned.1.call-done
  141.7 15.0 fusion.106
  156.8 10.5 reduce-scatter.16.cloned.1.call-done
  172.0 8.8 all-gather.20.cloned.1.call-done
  180.8 15.0 fusion.102
  195.9 10.5 reduce-scatter.18.cloned.1.call-done
  210.9 9.0 all-gather.22.cloned.1.call-done
  219.9 15.0 fusion.98
  235.0 10.5 reduce-scatter.20.cloned.1.call-done
  250.0 9.0 all-gather.24.cloned.1.call-done
  259.0 15.0 fusion.94
  274.1 10.5 reduce-scatter.22.cloned.1.call-done
  288.5 9.0 all-gather.26.cloned.1.call-done
  297.5 15.0 fusion.90
  314.4 4.6 fusion.88
  319.1 8.8 multiply_reduce_fusion.3
  334.9 3.6 all-gather.30.cloned.1.call-done
  338.5 60.6 %fusion.281 = (f32[4,256]{1,0:T(4,128)S(1)}, f32[4,256,25152]{1,2,0:T(8,128)}) fusion(bf16[4,256,768]{2,1,0:T(8,128)(2,1)} %all-gather.30.cloned.1.call-done, bf16[768,50304]{1,0:T(8,128)(2,1)} %param.21, s32[]{:T(128)S(6)} %select_n.3), kind=kOutput, calls=%fused_computation.310 | convolution fusion | flops 39586430976 | bytes 143331328 | tf_op jit(solution)/shard_map/bsd,dv->bsv/dot_general | solution.py:28
  399.1 65.9 %fusion.282 = (f32[4,256]{1,0:T(4,128)S(1)}, f32[4,256,25152]{1,2,0:T(8,128)}) fusion(bf16[4,256,1024]{2,1,0:T(8,128)(2,1)} %all-gather.28.cloned.1.call-done, bf16[1024,25152]{0,1:T(8,128)(2,1)} %param.16), kind=kOutput, calls=%fused_computation.311 | convolution fusion | flops 52773322752 | bytes 156635136 | tf_op jit(solution)/shard_map/bsd,dv->bsv/dot_general | solution.py:28
  467.6 61.1 %fusion.1 = (f32[4,256]{1,0:T(4,128)S(1)}, f32[4,256]{1,0:T(4,128)S(1)}) fusion(f32[4,256,25152]{1,2,0:T(8,128)} %get-tuple-element.60, f32[4,256]{1,0:T(4,128)S(1)} %get-tuple-element.51, f32[4,256,25152]{1,2,0:T(8,128)} %get-tuple-element.58, f32[4,256]{1,0:T(4,128)S(1)} %get-tuple-element.52), kind=kLoop, calls=%fused_computation.5 | loop fusion | flops 103020544 | bytes 206061568 | tf_op jit(solution)/shard_map/reduce_sum | solution.py:113
  528.7 2.5 psum.49
  531.2 81.4 %multiply_convert_fusion = (bf16[4,256,25152]{1,2,0:T(8,128)(2,1)}, f32[]{:T(128)}) fusion(f32[4,256,25152]{1,2,0:T(8,128)} %get-tuple-element.58, f32[4,256,25152]{1,2,0:T(8,128)} %get-tuple-element.60, f32[4,256]{1,0:T(4,128)S(1)} %get-tuple-element.49, f32[4,256]{1,0:T(4,128)S(1)} %get-tuple-element.50, f32[4,256]{1,0:T(4,128)S(1)} %get-tuple-element.52, ...), kind=kLoop, calls=%fused_computation | loop fusion | flops 283312128 | bytes 257576960 | tf_op jit(solution)/shard_map/convert_element_type | solution.py:119
  612.6 52.7 %convolution_bitcast_fusion = f32[768,25152]{0,1:T(8,128)} fusion(bf16[4,256,25152]{1,2,0:T(8,128)(2,1)} %get-tuple-element.39, bf16[4,256,768]{2,1,0:T(8,128)(2,1)S(1)} %copy-done.29), kind=kOutput, calls=%fused_computation.9 | convolution fusion | flops 39560675328 | bytes 130351104 | tf_op jit(solution)/shard_map/bsd,bsv->dv/dot_general | solution.py:28
  665.4 66.3 %fusion.5 = f32[4,256,768]{2,1,0:T(8,128)} fusion(bf16[4,256,25152]{1,2,0:T(8,128)(2,1)} %get-tuple-element.39, bf16[768,50304]{1,0:T(8,128)(2,1)} %param.21, s32[]{:T(128)S(6)} %select_n.3), kind=kOutput, calls=%fused_computation.10 | convolution fusion | flops 39560675328 | bytes 93388800 | tf_op jit(solution)/shard_map/bsv,dv->bsd/dot_general | solution.py:28
  731.8 1203.5 %all-reduce.5.cloned.1.call-done = f32[768,25152]{0,1:T(8,128)} async-done(((f32[768,25152]{0,1:T(8,128)}), f32[768,25152]{0,1:T(8,128)}) %all-reduce.5.cloned.1.call-update) | async-done | bytes 77266960 | tf_op jit(solution)/shard_map/psum | solution.py:121
  1936.6 4.7 all_to_all.4
  1944.7 2.6 convolution_bitcast_fusion.3
  1947.3 3.8 multiply_reduce_fusion.2
  1951.5 10.6 fusion.81
  1962.1 8.4 convolution_bitcast_fusion.2
  1971.4 8.5 convolution_bitcast_fusion.1
  1981.2 8.9 fusion.229
  1990.1 23.1 all-reduce
  2013.2 144.5 %all-gather.32.cloned.1.call-done = f32[768,50304]{0,1:T(8,128)} async-done(((f32[768,25152]{0,1:T(8,128)}), f32[768,50304]{0,1:T(8,128)}) %all-gather.32.cloned.1.call-update) | async-done | bytes 154533904 | tf_op jit(solution)/shard_map/all_gather | solution.py:121
  2157.7 152.3 %copy.28 = f32[768,50304]{1,0:T(8,128)} copy(f32[768,50304]{0,1:T(8,128)} %all-gather.32.cloned.1.call-done) | data formatting | bytes 309067776
  2310.0 115.7 %all-reduce.7.cloned.1.call-done = (f32[1,768,3072]{2,1,0:T(8,128)}, f32[1,3072,768]{2,1,0:T(8,128)}, f32[1,768,1024]{2,1,0:T(8,128)}) async-done(((f32[1,768,3072]{2,1,0:T(8,128)}, f32[1,3072,768]{2,1,0:T(8,128)}, f32[1,768,1024]{2,1,0:T(8,128)}), (f32[1,768,3072]{2,1,0:T(8,128)}, f32[1,3072,768]{2,1,0:T(8,128)}, f32[1,768,1024]{2,1,0:T(8,128)})) %all-reduce.7.cloned.1.call-update) | async-done | bytes 22020112 | tf_op jit(solution)/shard_map/psum | solution.py:125
  2425.7 8.8 copy.37
  2434.5 4.2 copy.38
  (167 shorter events, 55.5 us)
Async XLA Ops:
  7.2 1934.4 %copy-start = (bf16[1,768,1024]{2,1,0:T(8,128)(2,1)S(1)}, bf16[1,768,1024]{2,1,0:T(8,128)(2,1)}, u32[]{:S(2)}) copy-start(bf16[1,768,1024]{2,1,0:T(8,128)(2,1)} %param.20) | copy-start | bytes 4718596
  7.2 16.6 all-gather.12.cloned.1.call-start
  13.1 37.5 %reduce-scatter.10.cloned.1.call-start = ((), (), s32[]{:S(2)}) async-start(), calls=%async_computation.11 | async-start | bytes 6291456 | tf_op jit(solution)/shard_map/reduce_scatter | solution.py:93
  40.0 10.5 copy-start.5
  40.1 24.1 all-gather.14.cloned.1.call-start
  54.8 34.9 %reduce-scatter.12.cloned.1.call-start = ((), (), s32[]{:S(2)}) async-start(), calls=%async_computation.13 | async-start | bytes 6291456 | tf_op jit(solution)/shard_map/reduce_scatter | solution.py:93
  79.2 23.4 all-gather.16.cloned.1.call-start
  93.3 34.9 %reduce-scatter.14.cloned.1.call-start = ((), (), s32[]{:S(2)}) async-start(), calls=%async_computation.15 | async-start | bytes 6291456 | tf_op jit(solution)/shard_map/reduce_scatter | solution.py:93
  117.6 24.1 all-gather.18.cloned.1.call-start
  132.4 34.9 %reduce-scatter.16.cloned.1.call-start = ((), (), s32[]{:S(2)}) async-start(), calls=%async_computation.17 | async-start | bytes 6291456 | tf_op jit(solution)/shard_map/reduce_scatter | solution.py:93
  156.7 10.6 copy-start.9
  156.7 24.1 all-gather.20.cloned.1.call-start
  171.5 34.9 %reduce-scatter.18.cloned.1.call-start = ((), (), s32[]{:S(2)}) async-start(), calls=%async_computation.19 | async-start | bytes 6291456 | tf_op jit(solution)/shard_map/reduce_scatter | solution.py:93
  195.8 10.6 copy-start.11
  195.8 24.1 all-gather.22.cloned.1.call-start
  210.6 34.9 %reduce-scatter.20.cloned.1.call-start = ((), (), s32[]{:S(2)}) async-start(), calls=%async_computation.21 | async-start | bytes 6291456 | tf_op jit(solution)/shard_map/reduce_scatter | solution.py:93
  234.9 10.6 copy-start.13
  234.9 13.5 copy-start.27
  235.0 24.1 all-gather.24.cloned.1.call-start
  249.7 34.8 %reduce-scatter.22.cloned.1.call-start = ((), (), s32[]{:S(2)}) async-start(), calls=%async_computation.23 | async-start | bytes 6291456 | tf_op jit(solution)/shard_map/reduce_scatter | solution.py:93
  274.0 12.9 copy-start.26
  274.1 23.4 all-gather.26.cloned.1.call-start
  288.2 24.4 copy-start.28
  288.2 42.4 %reduce-scatter.24.cloned.1.call-start = ((), (), s32[]{:S(2)}) async-start(), calls=%async_computation.25 | async-start | bytes 6291456 | tf_op jit(solution)/shard_map/reduce_scatter | solution.py:93
  312.5 25.9 %all-gather.30.cloned.1.call-start = ((), (), s32[]{:S(2)}) async-start(), calls=%async_computation.27 | async-start | bytes 2359296 | tf_op jit(solution)/shard_map/all_gather | solution.py:106
  313.6 5.4 copy-start.20
  319.1 8.8 copy-start.30
  330.1 69.0 %all-gather.28.cloned.1.call-start = ((), (), s32[]{:S(2)}) async-start(), calls=%async_computation.26 | async-start | bytes 3145728 | tf_op jit(solution)/shard_map/all_gather | solution.py:98
  334.8 1600.5 %all-reduce.5.cloned.1.call-start = ((), (), s32[]{:S(2)}) async-start(), calls=%async_computation.29 | async-start | bytes 154533888 | tf_op jit(solution)/shard_map/psum | solution.py:121
  531.2 81.4 %copy-start.29 = (bf16[4,256,768]{2,1,0:T(8,128)(2,1)S(1)}, bf16[4,256,768]{2,1,0:T(8,128)(2,1)}, u32[]{:S(2)}) copy-start(bf16[4,256,768]{2,1,0:T(8,128)(2,1)} %all-gather.30.cloned.1.call-done) | copy-start | bytes 4718596
  665.4 1281.9 %reduce-scatter.26.cloned.1.call-start = ((), (), s32[]{:S(2)}) async-start(), calls=%async_computation.28 | async-start | bytes 4718592 | tf_op jit(solution)/shard_map/reduce_scatter | solution.py:123
  731.8 1425.9 %all-gather.32.cloned.1.call-start = ((), (), s32[]{:S(2)}) async-start(), calls=%async_computation.30 | async-start | bytes 231800832 | tf_op jit(solution)/shard_map/all_gather | solution.py:121
  1935.4 1.2 copy-start.7
  1935.4 6.2 copy-start.2
  1935.4 490.3 %all-reduce.7.cloned.1.call-start = ((), (), s32[]{:S(2)}) async-start(), calls=%async_computation.31 | async-start | bytes 44040192 | tf_op jit(solution)/shard_map/psum | solution.py:125
  1943.4 1.3 copy-start.1
  1943.4 4.0 copy-start.25
  1947.3 3.8 copy-start.4
  1947.3 24.1 slice-start.3
  1951.5 10.6 copy-start.17
  1951.5 10.6 copy-start.21
  1951.5 10.6 copy-start.23
  1951.5 19.9 slice-start.4
  1962.1 9.3 copy-start.19
  2425.7 8.8 slice-start
  2425.7 8.8 slice-start.1
  2425.7 8.8 slice-start.2
  2434.5 4.3 copy-start.18
  (10 other events, 9.8 us)
Sparse Core Ops, SparseCore 0:
  13.2 10.5 all-gather.11
  40.2 10.3 reduce-scatter.9
  54.9 9.1 all-gather.13
  79.3 10.3 reduce-scatter.11
  93.4 9.1 all-gather.15
  117.8 10.3 reduce-scatter.13
  132.5 9.1 all-gather.17
  156.9 10.3 reduce-scatter.15
  171.7 9.0 all-gather.19
  196.0 10.3 reduce-scatter.17
  210.8 9.0 all-gather.21
  235.1 10.3 reduce-scatter.19
  249.9 9.0 all-gather.23
  274.2 10.3 reduce-scatter.21
  288.3 9.1 all-gather.25
  312.7 10.3 reduce-scatter.23
  330.2 8.2 all-gather.29
  340.4 8.9 all-gather.27
  665.5 1269.8 all-reduce.4
  1938.0 9.0 reduce-scatter.25
  1948.6 209.0 all-gather.31
  2162.5 263.2 all-reduce.6
where the time goes:
time: 2460 us; the launch traced here: 2450 us
  waiting for transfers between devices  1610 us (65%)
  matrix products  425 us (17%)
  local copies, waits for them, and re-layouts  181 us (7%)
  other arithmetic  175 us (7%)
  blocking collectives  32.8 us (1%)
    psum x1, waiting for transfers between devices, local_step(): lax.psum(head_part, 'dp')  1200 us
    dot_general x22, matrix products, mat_mul(): jnp.einsum(subscripts, lhs_arr, rhs_arr, preferred_element_type=jnp.float32)  425 us
    unnamed x76, local copies, waits for them, and re-layouts  179 us
    all_gather x1, waiting for transfers between devices, local_step(): lax.all_gather(lax.psum(head_part, 'dp'), 'tp', axis=1, tiled=True)  144 us
    psum x1, waiting for transfers between devices, local_step(): lax.psum(local_grads, ('dp', 'tp'))  116 us
    convert_element_type x1, other arithmetic, local_step(): logit_grad = (kl_coef * (stud_prob - teach_prob)).astype(jnp.bfloat16)  81.4 us
    all_gather x8, waiting for transfers between devices, local_step(): gathered = lax.all_gather(normed, 'tp', axis=1, tiled=True)  73.5 us
    reduce_scatter x8, waiting for transfers between devices, local_step(): lax.psum_scatter(partial_out, 'tp', scatter_dimension=1, tiled=True)  73.4 us
  transfers between devices with their start and end apart: 22, of which 19 were waited for; matrix products, arithmetic and copies ran while one was open for 14% of the time, Pallas kernels for 0%

commit v1 on v0

v1 whole, which is shorter than its diff:
```python
import functools

import jax
import jax.numpy as jnp
from jax import lax
from jax.experimental import pallas as pl
from jax.experimental.pallas import tpu as pltpu
from jax.sharding import PartitionSpec as P


NORM_EPS = 1e-6
NEG = -3.0e38
BLK = 512
N_BLK = 50
N_OWN = 7
N_SHARED = 4 * N_OWN
OWN_SPLIT = (4, 3)
RED_SPLIT = (11, 11)
VMEM_LIMIT = 60 * 1024 * 1024


def rms_parts(values):
    vals32 = values.astype(jnp.float32)
    inv_rms = lax.rsqrt(jnp.mean(vals32 * vals32, axis=-1, keepdims=True) + NORM_EPS)
    return vals32 * inv_rms, inv_rms


def rms_back(normed, inv_rms, grad_out):
    return inv_rms * (grad_out - normed * jnp.mean(grad_out * normed, axis=-1, keepdims=True))


def gelu_tanh(values):
    return jax.nn.gelu(values, approximate=True)


def gelu_back(pre_act, grad_out):
    return jax.vjp(gelu_tanh, pre_act)[1](grad_out)[0]


def mat_mul(subscripts, lhs_arr, rhs_arr):
    return jnp.einsum(subscripts, lhs_arr, rhs_arr, preferred_element_type=jnp.float32)


def dot_f32(lhs, rhs):
    return jnp.dot(lhs, rhs, preferred_element_type=jnp.float32)


def dot_rows(lhs, rhs):
    return lax.dot_general(lhs, rhs, (((1,), (1,)), ((), ())), preferred_element_type=jnp.float32)


def valid_cols(core, blk, half_cols):
    cols = blk * BLK + lax.broadcasted_iota(jnp.int32, (1, BLK), 1)
    return (cols >= 64 * core) & (cols < half_cols + 64 * core)


def stats_kernel(half_cols, meta, ht, rs, wt, ws, zt_out, zs_out, st_out, mt, st, at, ms, ss):
    blk = pl.program_id(0)
    valid = valid_cols(meta[0], blk, half_cols)

    @pl.when(blk == 0)
    def _():
        mt[...] = jnp.full_like(mt, NEG)
        ms[...] = jnp.full_like(ms, NEG)
        st[...] = jnp.zeros_like(st)
        at[...] = jnp.zeros_like(at)
        ss[...] = jnp.zeros_like(ss)

    rows_all = ht.shape[0]
    step = 512
    for row in range(0, rows_all, step):
        rows = pl.ds(row, step)
        zt = jnp.where(valid, dot_rows(ht[rows, :], wt[...]), NEG)
        zs = jnp.where(valid, dot_f32(rs[rows, :], ws[...]), NEG)
        zt_out[rows, :] = zt
        zs_out[rows, :] = zs
        parts_t = [zt[:, j:j + 128] for j in range(0, BLK, 128)]
        parts_s = [zs[:, j:j + 128] for j in range(0, BLK, 128)]
        m_old = mt[rows, :]
        m_new = functools.reduce(jnp.maximum, parts_t, m_old)
        corr = jnp.exp(m_old - m_new)
        exps = [jnp.exp(p - m_new) for p in parts_t]
        st[rows, :] = st[rows, :] * corr + sum(exps)
        at[rows, :] = at[rows, :] * corr + sum(e * (p - q) for e, p, q in zip(exps, parts_t, parts_s))
        mt[rows, :] = m_new
        m_old = ms[rows, :]
        m_new = functools.reduce(jnp.maximum, parts_s, m_old)
        corr = jnp.exp(m_old - m_new)
        ss[rows, :] = ss[rows, :] * corr + sum(jnp.exp(p - m_new) for p in parts_s)
        ms[rows, :] = m_new

    @pl.when(blk == pl.num_programs(0) - 1)
    def _():
        top_t = jnp.max(mt[...], axis=-1, keepdims=True)
        scale = jnp.exp(mt[...] - top_t)
        sum_t = jnp.sum(st[...] * scale, axis=-1, keepdims=True)
        sum_a = jnp.sum(at[...] * scale, axis=-1, keepdims=True)
        top_s = jnp.max(ms[...], axis=-1, keepdims=True)
        sum_s = jnp.sum(ss[...] * jnp.exp(ms[...] - top_s), axis=-1, keepdims=True)
        lane = lax.broadcasted_iota(jnp.int32, st_out.shape, 1)
        res = jnp.where(lane == 0, top_t, jnp.where(lane == 1, sum_t, sum_a))
        res = jnp.where(lane == 3, top_s, jnp.where(lane == 4, sum_s, res))
        st_out[...] = res


def head_stats(meta, ht, rs, hts, head_s, half_cols):
    rows, d_t = ht.shape
    d_s = rs.shape[1]
    cols = N_BLK * BLK
    grid_spec = pltpu.PrefetchScalarGridSpec(
        num_scalar_prefetch=1,
        grid=(N_BLK,),
        in_specs=[
            pl.BlockSpec((rows, d_t), lambda k, m: (0, 0), pipeline_mode=pl.Buffered(1)),
            pl.BlockSpec((rows, d_s), lambda k, m: (0, 0), pipeline_mode=pl.Buffered(1)),
            pl.BlockSpec((BLK, d_t), lambda k, m: (k, 0)),
            pl.BlockSpec((d_s, BLK), lambda k, m: (0, k + (N_BLK - 1) * m[0])),
        ],
        out_specs=[
            pl.BlockSpec((rows, BLK), lambda k, m: (0, k)),
            pl.BlockSpec((rows, BLK), lambda k, m: (0, k)),
            pl.BlockSpec((rows, 128), lambda k, m: (0, 0)),
        ],
        scratch_shapes=[pltpu.VMEM((rows, 128), jnp.float32)] * 5,
    )
    return pl.pallas_call(
        functools.partial(stats_kernel, half_cols),
        grid_spec=grid_spec,
        out_shape=[
            jax.ShapeDtypeStruct((rows, cols), jnp.float32),
            jax.ShapeDtypeStruct((rows, cols), jnp.float32),
            jax.ShapeDtypeStruct((rows, 128), jnp.float32),
        ],
        compiler_params=pltpu.CompilerParams(dimension_semantics=("arbitrary",), vmem_limit_bytes=VMEM_LIMIT),
        cost_estimate=pl.CostEstimate(
            flops=2 * rows * cols * (d_t + d_s), bytes_accessed=cols * (2 * (d_t + d_s) + 8 * rows),
            transcendentals=2 * rows * cols),
        name="head_stats",
    )(meta, ht, rs, hts, head_s)


def logit_grad(zt, zs, lse_t, lse_s, coef):
    return (coef * (jnp.exp(zs - lse_s) - jnp.exp(zt - lse_t))).astype(jnp.bfloat16)


def grad_kernel(half_cols, coef, meta, ht, rs, rst, lt, ls, wt, ws, zt_own, zs_own, out):
    own = meta[1]
    valid = valid_cols(meta[0], meta[2] + pl.program_id(0), half_cols)
    lg = logit_grad(zt_own[...], zs_own[...], lt[own], ls[own], coef)
    out[...] = dot_f32(rst[own], lg)
    for other in range(1, 4):
        grp = lax.rem(own + other, 4)
        zt = jnp.where(valid, dot_rows(ht[grp], wt[...]), NEG)
        zs = jnp.where(valid, dot_f32(rs[grp], ws[...]), NEG)
        out[...] += dot_f32(rst[grp], logit_grad(zt, zs, lt[grp], ls[grp], coef))


def head_grad_blocks(n_blocks, meta, ht_all, rs_all, rst_all, lse_t, lse_s, hts, head_s, zt, zs, half_cols, coef):
    groups, rows, d_t = ht_all.shape
    d_s = rs_all.shape[2]

    def whole(shape):
        return pl.BlockSpec(shape, lambda i, m: (0,) * len(shape), pipeline_mode=pl.Buffered(1))

    grid_spec = pltpu.PrefetchScalarGridSpec(
        num_scalar_prefetch=1,
        grid=(n_blocks,),
        in_specs=[
            whole((groups, rows, d_t)),
            whole((groups, rows, d_s)),
            whole((groups, d_s, rows)),
            whole((groups, rows, 1)),
            whole((groups, rows, 1)),
            pl.BlockSpec((BLK, d_t), lambda i, m: (m[2] + i, 0)),
            pl.BlockSpec((d_s, BLK), lambda i, m: (0, m[2] + i + (N_BLK - 1) * m[0])),
            pl.BlockSpec((rows, BLK), lambda i, m: (0, m[2] + i)),
            pl.BlockSpec((rows, BLK), lambda i, m: (0, m[2] + i)),
        ],
        out_specs=pl.BlockSpec((d_s, BLK), lambda i, m: (0, i)),
    )
    cols = n_blocks * BLK
    return pl.pallas_call(
        functools.partial(grad_kernel, half_cols, coef),
        grid_spec=grid_spec,
        out_shape=jax.ShapeDtypeStruct((d_s, cols), jnp.float32),
        compiler_params=pltpu.CompilerParams(dimension_semantics=("arbitrary",), vmem_limit_bytes=VMEM_LIMIT),
        cost_estimate=pl.CostEstimate(
            flops=2 * rows * cols * (3 * d_t + 7 * d_s), bytes_accessed=cols * (2 * d_t + 6 * d_s + 8 * rows),
            transcendentals=8 * rows * cols),
        name="head_grad",
    )(meta, ht_all, rs_all, rst_all, lse_t, lse_s, hts, head_s, zt, zs)


def input_grad_kernel(coef, meta, lt, ls, zt, zs, ws, out):
    blk = pl.program_id(0)
    last = pl.num_programs(0) - 1

    @pl.when(blk == 0)
    def _():
        out[...] = jnp.zeros_like(out)

    @pl.when(blk < last)
    def _():
        lg = logit_grad(zt[...], zs[...], lt[...], ls[...], coef)
        out[...] += dot_rows(lg, ws[...])

    @pl.when(blk == last)
    def _():
        lg = logit_grad(zt[:, :128], zs[:, :128], lt[...], ls[...], coef)
        out[...] += dot_rows(lg, ws[:, :128])


def head_input_grad(meta, lse_t, lse_s, zt, zs, head_s, coef):
    rows = zt.shape[0]
    d_s = head_s.shape[0]
    cols = N_BLK * BLK
    grid_spec = pltpu.PrefetchScalarGridSpec(
        num_scalar_prefetch=1,
        grid=(N_BLK,),
        in_specs=[
            pl.BlockSpec((rows, 1), lambda k, m: (0, 0)),
            pl.BlockSpec((rows, 1), lambda k, m: (0, 0)),
            pl.BlockSpec((rows, BLK), lambda k, m: (0, k)),
            pl.BlockSpec((rows, BLK), lambda k, m: (0, k)),
            pl.BlockSpec((d_s, BLK), lambda k, m: (0, k + (N_BLK - 1) * m[0])),
        ],
        out_specs=pl.BlockSpec((rows, d_s), lambda k, m: (0, 0)),
    )
    return pl.pallas_call(
        functools.partial(input_grad_kernel, coef),
        grid_spec=grid_spec,
        out_shape=jax.ShapeDtypeStruct((rows, d_s), jnp.float32),
        compiler_params=pltpu.CompilerParams(dimension_semantics=("arbitrary",), vmem_limit_bytes=VMEM_LIMIT),
        cost_estimate=pl.CostEstimate(
            flops=4 * rows * cols * d_s, bytes_accessed=cols * (2 * d_s + 8 * rows), transcendentals=2 * rows * cols),
        name="head_input_grad",
    )(meta, lse_t, lse_s, zt, zs, head_s)


def block_pieces():
    shared = []
    for part, n_blocks in enumerate(OWN_SPLIT):
        for j in range(n_blocks):
            shared.append((part, j))
    pieces = {}
    for k in range(N_SHARED):
        part, j = shared[k % N_OWN]
        pieces[k] = (part, k // N_OWN, j * BLK)
    k = N_SHARED
    for part, n_blocks in enumerate(RED_SPLIT):
        for j in range(n_blocks):
            pieces[k] = (len(OWN_SPLIT) + part, None, j * BLK)
            k += 1
    return pieces


def piece_view(refs, piece, extra, width):
    part, lead, col = piece
    ref = refs[part]
    if lead is None:
        return ref.at[:, pl.ds(col + extra, width)]
    return ref.at[lead, :, pl.ds(col + extra, width)]


def assemble_kernel(n_arr, n_buf, meta, *refs):
    own, partner = refs[:n_arr], refs[n_arr:2 * n_arr]
    out, bufs, seam_a, seam_b, in_sem, out_sem, seam_sem = refs[2 * n_arr:]
    core = meta[0]
    pieces = block_pieces()
    seam_col = (N_BLK - 1) * BLK
    jobs = [(0, pieces[k], 0, k * BLK, BLK) for k in range(N_BLK - 1)]
    jobs.append((1, pieces[0], 128, seam_col + 128, BLK - 128))
    jobs += [(1, pieces[k], 0, seam_col + k * BLK, BLK) for k in range(1, N_BLK - 1)]
    jobs.append((1, pieces[N_BLK - 1], 0, seam_col + (N_BLK - 1) * BLK, 128))

    def fetch(half, piece, extra, width, dst, sem):
        @pl.when(core == half)
        def _():
            pltpu.make_async_copy(piece_view(own, piece, extra, width), dst, sem).start()

        @pl.when(core != half)
        def _():
            pltpu.make_async_copy(piece_view(partner, piece, extra, width), dst, sem).start()

    fetch(0, pieces[N_BLK - 1], 0, 128, seam_a, seam_sem.at[0])
    fetch(1, pieces[0], 0, 128, seam_b, seam_sem.at[1])

    def buf_of(i):
        return bufs.at[i % n_buf, :, pl.ds(0, jobs[i][4])]

    def start_in(i):
        half, piece, extra, _, width = jobs[i]
        fetch(half, piece, extra, width, buf_of(i), in_sem.at[i % n_buf])

    def out_copy(i):
        return pltpu.make_async_copy(buf_of(i), out.at[:, pl.ds(jobs[i][3], jobs[i][4])], out_sem.at[i % n_buf])

    def finish_in(i):
        pltpu.make_async_copy(buf_of(i), buf_of(i), in_sem.at[i % n_buf]).wait()
        out_copy(i).start()

    lag = n_buf // 2
    for i in range(len(jobs) + lag):
        if i < len(jobs):
            if i >= n_buf:
                out_copy(i - n_buf).wait()
            start_in(i)
        if i >= lag:
            finish_in(i - lag)
    pltpu.make_async_copy(seam_a, seam_a, seam_sem.at[0]).wait()
    pltpu.make_async_copy(seam_b, seam_b, seam_sem.at[1]).wait()
    seam_a[...] += seam_b[...]
    seam = pltpu.make_async_copy(seam_a, out.at[:, pl.ds(seam_col, 128)], seam_sem.at[0])
    seam.start()
    for i in range(len(jobs) - n_buf, len(jobs)):
        out_copy(i).wait()
    seam.wait()


def assemble(meta, own, partner, vocab):
    d_s = own[0].shape[-2]
    n_buf = 8
    any_spec = pl.BlockSpec(memory_space=pl.ANY)
    return pl.pallas_call(
        functools.partial(assemble_kernel, len(own), n_buf),
        in_specs=[pl.BlockSpec(memory_space=pltpu.SMEM)] + [any_spec] * (2 * len(own)),
        out_specs=any_spec,
        out_shape=jax.ShapeDtypeStruct((d_s, vocab), jnp.float32),
        scratch_shapes=[
            pltpu.VMEM((n_buf, d_s, BLK), jnp.float32),
            pltpu.VMEM((d_s, 128), jnp.float32),
            pltpu.VMEM((d_s, 128), jnp.float32),
            pltpu.SemaphoreType.DMA((n_buf,)),
            pltpu.SemaphoreType.DMA((n_buf,)),
            pltpu.SemaphoreType.DMA((2,)),
        ],
        compiler_params=pltpu.CompilerParams(vmem_limit_bytes=VMEM_LIMIT),
        cost_estimate=pl.CostEstimate(flops=d_s * vocab * 100, bytes_accessed=8 * d_s * vocab, transcendentals=0),
        name="assemble",
    )(meta, *own, *partner)


def after(value, *earlier):
    return lax.optimization_barrier((value, *earlier))[0]


def solution(mesh):
    dp_size = mesh.shape['dp']
    tp_size = mesh.shape['tp']
    swap = [(0, 1), (1, 0)]

    def local_step(x_teach, x_stud, w_up_t, w_down_t, gain_t, head_t, w_up_s, w_down_s, gain_s, proj_s, head_s):
        dp_idx = lax.axis_index('dp')
        core = lax.axis_index('tp')
        n_seq, seq_len, d_s = x_stud.shape
        d_t = x_teach.shape[-1]
        local_tok = n_seq * seq_len
        group_tok = local_tok * tp_size
        n_tokens = group_tok * dp_size
        half_cols = head_t.shape[1]
        vocab = head_s.shape[1]
        feat_coef = 1.0 / (n_tokens * d_t)
        kl_coef = 1.0 / n_tokens
        w_up, w_down, gain, proj = w_up_s[0], w_down_s[0], gain_s[0], proj_s[0]
        both = ('dp', 'tp')

        x_all = lax.all_gather(x_stud.reshape(local_tok, d_s), both, axis=0, tiled=True)
        norm_all, _ = rms_parts(x_all)
        n_all = (norm_all * gain).astype(jnp.bfloat16)

        norm_cur, _ = rms_parts(x_stud.reshape(local_tok, d_s))
        normed = (norm_cur * gain).astype(jnp.bfloat16)
        hidden_s = gelu_tanh(mat_mul('sd,df->sf', normed, w_up)).astype(jnp.bfloat16)
        residual = x_stud.reshape(local_tok, d_s).astype(jnp.float32) + mat_mul('sf,fd->sd', hidden_s, w_down)
        norm_next, inv_next = rms_parts(residual)
        proj_in = norm_next.astype(jnp.bfloat16)
        proj_out = mat_mul('sd,de->se', proj_in, proj)
        rs_flat = lax.all_gather(proj_in, both, axis=0, tiled=True)
        rs_all = rs_flat.reshape(dp_size, group_tok, d_s)
        rst_all = jnp.swapaxes(rs_all, 1, 2)
        rs_grp = lax.dynamic_index_in_dim(rs_all, dp_idx, 0, keepdims=False)

        padded = jnp.pad(head_t.T, ((64, N_BLK * BLK - half_cols), (0, 0)))
        hts = lax.dynamic_slice_in_dim(padded, 64 - 64 * core, N_BLK * BLK, axis=0)

        f_half = w_up.shape[1] // tp_size
        up_half = lax.dynamic_slice_in_dim(w_up, core * f_half, f_half, axis=1)
        down_half = lax.dynamic_slice_in_dim(w_down, core * f_half, f_half, axis=0)
        pre_half = mat_mul('sd,df->sf', n_all, up_half)
        act_half = gelu_tanh(pre_half).astype(jnp.bfloat16)

        hidden = x_teach
        for layer_idx in range(w_up_t.shape[0]):
            t_in = (rms_parts(hidden)[0] * gain_t[layer_idx]).astype(jnp.bfloat16)
            gathered = lax.all_gather(t_in, 'tp', axis=1, tiled=True)
            hidden_act = gelu_tanh(mat_mul('bsd,df->bsf', gathered, w_up_t[layer_idx])).astype(jnp.bfloat16)
            partial_out = mat_mul('bsf,fd->bsd', hidden_act, w_down_t[layer_idx])
            layer_out = lax.psum_scatter(partial_out, 'tp', scatter_dimension=1, tiled=True)
            hidden = hidden + layer_out.astype(jnp.bfloat16)
        feature = lax.all_to_all(hidden, 'tp', 0, 1, tiled=True)
        final_norm = rms_parts(hidden)[0].astype(jnp.bfloat16)
        ht_grp = lax.all_gather(final_norm, 'tp', axis=1, tiled=True).reshape(group_tok, d_t)
        ht_all = lax.all_gather(ht_grp, 'dp')

        meta0 = jnp.stack([core, dp_idx, jnp.int32(0)]).astype(jnp.int32)
        zt, zs, stats = head_stats(meta0, ht_grp, rs_grp, hts, head_s, half_cols)
        stats_all = lax.all_gather(stats[:, :8].T, both).reshape(dp_size, tp_size, 8, group_tok)
        top_t, sum_t, sum_a, top_s, sum_s = [stats_all[:, :, j, :] for j in range(5)]
        max_t = jnp.max(top_t, axis=1)
        max_s = jnp.max(top_s, axis=1)
        scale_t = jnp.exp(top_t - max_t[:, None])
        all_t = jnp.sum(sum_t * scale_t, axis=1)
        all_a = jnp.sum(sum_a * scale_t, axis=1)
        all_s = jnp.sum(sum_s * jnp.exp(top_s - max_s[:, None]), axis=1)
        lse_t = max_t + jnp.log(all_t)
        lse_s = max_s + jnp.log(all_s)
        kl_total = jnp.sum(all_a / all_t - lse_t + lse_s)
        lse_t = lse_t[..., None]
        lse_s = lse_s[..., None]

        def blocks(base, count, lse):
            meta = jnp.stack([core, dp_idx, base]).astype(jnp.int32)
            return head_grad_blocks(count, meta, ht_all, rs_all, rst_all, lse, lse_s, hts, head_s, zt, zs,
                                    half_cols, kl_coef)

        own_parts = []
        base, lse_o = dp_idx * N_OWN, lse_t
        for count in OWN_SPLIT:
            own_parts.append(blocks(base, count, lse_o))
            base = base + count
            lse_o = after(lse_t, own_parts[-1])
        shared = []
        for part in own_parts:
            shared.append(lax.all_gather(part, 'dp'))

        lse_own_t = lax.dynamic_index_in_dim(lse_o, dp_idx, 0, keepdims=False)
        lse_own_s = lax.dynamic_index_in_dim(lse_s, dp_idx, 0, keepdims=False)
        full_in_grad = head_input_grad(meta0, lse_own_t, lse_own_s, zt, zs, head_s, kl_coef)
        give = lax.dynamic_slice_in_dim(full_in_grad, (1 - core) * local_tok, local_tok, axis=0)
        keep = lax.dynamic_slice_in_dim(full_in_grad, core * local_tok, local_tok, axis=0)
        head_in_grad = keep + lax.ppermute(give, 'tp', swap)

        feat_err = proj_out - feature.reshape(local_tok, d_t)
        err_total = jnp.sum(feat_err * feat_err)
        err_grad = (2.0 * feat_coef * feat_err).astype(jnp.bfloat16)
        out_grad = mat_mul('se,de->sd', err_grad, proj)
        resid_grad = rms_back(norm_next, inv_next, out_grad + head_in_grad)
        resid_all = lax.all_gather(resid_grad.astype(jnp.bfloat16), both, axis=0, tiled=True)
        err_all = lax.all_gather(err_grad, both, axis=0, tiled=True)

        lse_r = after(lse_t, full_in_grad)
        redundant = []
        base = jnp.int32(N_SHARED)
        for count in RED_SPLIT:
            redundant.append(blocks(base, count, lse_r))
            base = base + count
            lse_r = after(lse_t, redundant[-1])
        own = shared + redundant
        partner = []
        for part in own:
            partner.append(lax.ppermute(part, 'tp', swap))

        resid_all = after(resid_all, redundant[-1])
        act_grad = mat_mul('sd,fd->sf', resid_all, down_half)
        pre_grad = gelu_back(pre_half, act_grad).astype(jnp.bfloat16)
        up_part = mat_mul('sd,sf->df', n_all, pre_grad)
        down_part = mat_mul('sf,sd->fd', act_half, resid_all)
        e_half = d_t // tp_size
        proj_part = mat_mul('sd,se->de', rs_flat, lax.dynamic_slice_in_dim(err_all, core * e_half, e_half, axis=1))
        pre_own = lax.dynamic_slice_in_dim(pre_grad, dp_idx * group_tok, group_tok, axis=0)
        norm_own = lax.dynamic_slice_in_dim(norm_all, dp_idx * group_tok, group_tok, axis=0)
        gain_part = jnp.sum(mat_mul('sf,df->sd', pre_own, up_half) * norm_own, axis=0)

        grad_up = lax.all_gather(up_part, 'tp', axis=1, tiled=True)[None]
        grad_down = lax.all_gather(down_part, 'tp', axis=0, tiled=True)[None]
        grad_proj = lax.all_gather(proj_part, 'tp', axis=1, tiled=True)[None]
        grad_gain, err_sum = lax.psum((gain_part, err_total), both)
        loss = feat_coef * err_sum + kl_coef * kl_total
        head_grad = assemble(meta0, own, partner, vocab)
        return loss, grad_up, grad_down, grad_gain[None], grad_proj, head_grad

    in_specs = (P('dp', 'tp', None), P(('dp', 'tp'), None, None), P(None, None, 'tp'), P(None, 'tp', None),
                P(), P(None, 'tp'), P(), P(), P(), P(), P())
    out_specs = (P(), P(), P(), P(), P(), P())

    return jax.shard_map(local_step, mesh=mesh, in_specs=in_specs, out_specs=out_specs, check_vma=False)
```

time: 2460 us -> 1330 us (0.54)
  waiting for transfers between devices: 1610 us -> 162 us
  Pallas kernels: 0 us -> 700 us
  matrix products: 425 us -> 241 us
  other arithmetic: 175 us -> 51.3 us
  local copies, waits for them, and re-layouts: 181 us -> 86.7 us
  blocking collectives: 32.8 us -> 60.1 us
    psum x2 -> x0, waiting for transfers between devices: 1320 us -> none  [the longest x1 1200 us: local_step(): lax.psum(head_part, 'dp')]
    pallas_call x0 -> x7, Pallas kernels: none -> 700 us  [the longest x4 350 us: head_grad_blocks(): pl.pallas_call(functools.partial(grad_kernel, half_cols, coef), grid_spec...]
    dot_general x22 -> x19, matrix products: 425 us -> 241 us  [mat_mul(): jnp.einsum(subscripts, lhs_arr, rhs_arr, preferred_element_type=jnp.float32)]
    unnamed x76 -> x71, local copies, waits for them, and re-layouts: 179 us -> 22.5 us
    all_gather x11 -> x19, waiting for transfers between devices: 222 us -> 73.2 us  [the longest x8 73.1 us: local_step(): gathered = lax.all_gather(t_in, 'tp', axis=1, tiled=True)]
    convert_element_type x11, other arithmetic: 94.3 us -> 14.8 us  [the longest x8 11.4 us: local_step(): t_in = (rms_parts(hidden)[0] * gain_t[layer_idx]).astype(jnp.bfloat16)]
    reduce_sum x1 -> x2, other arithmetic: 61.1 us -> 0.78 us  [the longest x1 0.59 us: local_step(): kl_total = jnp.sum(all_a / all_t - lse_t + lse_s)]
    dynamic_slice x0 -> x2, local copies, waits for them, and re-layouts: none -> 37.6 us  [the longest x1 35 us: local_step(): hts = lax.dynamic_slice_in_dim(padded, 64 - 64 * core, N_BLK * BLK, axis=0)]
  transfers between devices with their start and end apart: 22 -> 32, of which waited for: 19 -> 17; matrix products, arithmetic and copies ran while one was open for 14% -> 15% of each run, Pallas kernels for 0% -> 45%
where the time goes in v1:
time: 1330 us; the launch traced here: 1320 us
  Pallas kernels  700 us (53%)
  matrix products  241 us (18%)
  waiting for transfers between devices  162 us (12%)
  local copies, waits for them, and re-layouts  86.7 us (7%)
  blocking collectives  60.1 us (5%)
  other arithmetic  51.3 us (4%)
  between operations  17.7 us (1%)
    pallas_call x4, Pallas kernels, head_grad_blocks(): pl.pallas_call(functools.partial(grad_kernel, half_cols, coef), grid_spec...  350 us
    dot_general x19, matrix products, mat_mul(): jnp.einsum(subscripts, lhs_arr, rhs_arr, preferred_element_type=jnp.float32)  241 us
    pallas_call x1, Pallas kernels, head_stats(): pl.pallas_call(functools.partial(stats_kernel, half_cols), grid_spec=grid...  146 us
    pallas_call x1, Pallas kernels, head_input_grad(): pl.pallas_call(functools.partial(input_grad_kernel, coef), grid_spec=grid...  105 us
    pallas_call x1, Pallas kernels, assemble(): pl.pallas_call(functools.partial(assemble_kernel, len(own), n_buf), in_sp...  99.1 us
    reduce_scatter x8, waiting for transfers between devices, local_step(): lax.psum_scatter(partial_out, 'tp', scatter_dimension=1, tiled=True)  82.5 us
    all_gather x8, waiting for transfers between devices, local_step(): gathered = lax.all_gather(t_in, 'tp', axis=1, tiled=True)  73.1 us
    psum x1, blocking collectives, local_step(): grad_gain, err_sum = lax.psum((gain_part, err_total), both)  41.2 us
  transfers between devices with their start and end apart: 32, of which 17 were waited for; matrix products, arithmetic and copies ran while one was open for 15% of the time, Pallas kernels for 45%

profile of v1, /device:TPU:0, one launch (start us, length us, event | category | flops | bytes accessed | tf_op | source)
XLA Modules:
  0.0 1323.0 jit_solution(13268022581448576133)
XLA Ops:
  13.0 10.7 all-gather.23.cloned.1.call-done
  23.7 6.9 fusion.115
  30.6 9.4 fusion.113
  40.1 10.5 reduce-scatter.9.cloned.1.call-done
  55.2 8.9 all-gather.25.cloned.1.call-done
  64.1 15.0 %fusion.109 = f32[4,256,1024]{2,1,0:T(8,128)} fusion(bf16[8,2048,1024]{2,1,0:T(8,128)(2,1)} %param.14, bf16[4,256,1024]{2,1,0:T(8,128)(2,1)} %all-gather.25.cloned.1.call-done, bf16[8,1024,2048]{2,1,0:T(8,128)(2,1)} %param.13), kind=kOutput, calls=%fused_computation.125 | convolution fusion | flops 8608808960 | bytes 14680064 | tf_op jit(solution)/shard_map/bsf,fd->bsd/dot_general | solution.py:41
  79.2 10.5 reduce-scatter.11.cloned.1.call-done
  93.9 8.7 all-gather.27.cloned.1.call-done
  102.6 15.0 %fusion.105 = f32[4,256,1024]{2,1,0:T(8,128)} fusion(bf16[8,2048,1024]{2,1,0:T(8,128)(2,1)} %param.14, bf16[4,256,1024]{2,1,0:T(8,128)(2,1)} %all-gather.27.cloned.1.call-done, bf16[8,1024,2048]{2,1,0:T(8,128)(2,1)} %param.13), kind=kOutput, calls=%fused_computation.121 | convolution fusion | flops 8608808960 | bytes 14680064 | tf_op jit(solution)/shard_map/bsf,fd->bsd/dot_general | solution.py:41
  117.7 10.5 reduce-scatter.13.cloned.1.call-done
  132.7 9.0 all-gather.29.cloned.1.call-done
  141.7 15.0 %fusion.101 = f32[4,256,1024]{2,1,0:T(8,128)} fusion(bf16[8,2048,1024]{2,1,0:T(8,128)(2,1)} %param.14, bf16[4,256,1024]{2,1,0:T(8,128)(2,1)} %all-gather.29.cloned.1.call-done, bf16[8,1024,2048]{2,1,0:T(8,128)(2,1)} %param.13), kind=kOutput, calls=%fused_computation.117 | convolution fusion | flops 8608808960 | bytes 14680064 | tf_op jit(solution)/shard_map/bsf,fd->bsd/dot_general | solution.py:41
  156.8 10.5 reduce-scatter.15.cloned.1.call-done
  171.8 9.0 all-gather.31.cloned.1.call-done
  180.8 15.0 %fusion.97 = f32[4,256,1024]{2,1,0:T(8,128)} fusion(bf16[8,2048,1024]{2,1,0:T(8,128)(2,1)} %param.14, bf16[4,256,1024]{2,1,0:T(8,128)(2,1)} %all-gather.31.cloned.1.call-done, bf16[8,1024,2048]{2,1,0:T(8,128)(2,1)} %param.13), kind=kOutput, calls=%fused_computation.113 | convolution fusion | flops 8608808960 | bytes 14680064 | tf_op jit(solution)/shard_map/bsf,fd->bsd/dot_general | solution.py:41
  195.9 10.5 reduce-scatter.17.cloned.1.call-done
  210.9 9.0 all-gather.33.cloned.1.call-done
  219.9 15.0 %fusion.93 = f32[4,256,1024]{2,1,0:T(8,128)} fusion(bf16[8,2048,1024]{2,1,0:T(8,128)(2,1)} %param.14, bf16[4,256,1024]{2,1,0:T(8,128)(2,1)} %all-gather.33.cloned.1.call-done, bf16[8,1024,2048]{2,1,0:T(8,128)(2,1)} %param.13), kind=kOutput, calls=%fused_computation.109 | convolution fusion | flops 8608808960 | bytes 14680064 | tf_op jit(solution)/shard_map/bsf,fd->bsd/dot_general | solution.py:41
  235.0 10.5 reduce-scatter.19.cloned.1.call-done
  250.2 8.8 all-gather.35.cloned.1.call-done
  259.0 15.0 %fusion.89 = f32[4,256,1024]{2,1,0:T(8,128)} fusion(bf16[8,2048,1024]{2,1,0:T(8,128)(2,1)} %param.14, bf16[4,256,1024]{2,1,0:T(8,128)(2,1)} %all-gather.35.cloned.1.call-done, bf16[8,1024,2048]{2,1,0:T(8,128)(2,1)} %param.13), kind=kOutput, calls=%fused_computation.105 | convolution fusion | flops 8608808960 | bytes 14680064 | tf_op jit(solution)/shard_map/bsf,fd->bsd/dot_general | solution.py:41
  274.1 10.5 reduce-scatter.21.cloned.1.call-done
  289.1 9.0 all-gather.37.cloned.1.call-done
  298.1 15.0 %fusion.85 = f32[4,256,1024]{2,1,0:T(8,128)} fusion(bf16[8,2048,1024]{2,1,0:T(8,128)(2,1)} %param.14, bf16[4,256,1024]{2,1,0:T(8,128)(2,1)} %all-gather.37.cloned.1.call-done, bf16[8,1024,2048]{2,1,0:T(8,128)(2,1)} %param.13), kind=kOutput, calls=%fused_computation.101 | convolution fusion | flops 8608808960 | bytes 14680064 | tf_op jit(solution)/shard_map/bsf,fd->bsd/dot_general | solution.py:41
  314.6 9.1 reduce-scatter.23.cloned.1.call-done
  327.5 8.1 fusion.80
  335.6 6.0 multiply_reduce_fusion.3
  345.1 4.6 all_to_all.4
  352.7 35.0 %pad_dynamic-slice_fusion.wt = bf16[25600,1024]{1,0:T(8,128)(2,1)} fusion(s32[]{:T(128)S(6)} %select_n.26, bf16[25152,1024]{1,0:T(8,128)(2,1)} %bitcast.219), kind=kLoop, calls=%fused_computation | loop fusion | bytes 103940096 | tf_op jit(solution)/shard_map/dynamic_slice | solution.py:384
  389.0 8.8 copy.58
  400.5 145.6 %head_stats.1 = (f32[1024,25600]{1,0:T(8,128)}, f32[1024,25600]{1,0:T(8,128)}, f32[1024,128]{1,0:T(8,128)}) custom-call(s32[3]{0:T(128)} %get-tuple-element.69.meta, bf16[1024,1024]{1,0:T(8,128)(2,1)} %bitcast.235, bf16[1024,768]{1,0:T(8,128)(2,1)} %dynamic-slice_bitcast_fusion.rs, bf16[25600,1024]{1,0:T(8,128)(2,1)} %pad_dynamic-slice_fusion.wt, ...), custom_call_target="tpu_custom_call" | custom-call | flops 93952409600 | bytes 301465600 | tf_op jit(solution)/shard_map/head_stats/pallas_call | solution.py:126
  547.3 14.3 %all-gather = f32[64,1024]{1,0:T(8,128)S(1)} all-gather(f32[8,1024]{1,0:T(8,128)S(1)} %copy.56), channel_id=2, replica_groups=mesh['dp'=4,'tp'=2] {'dp','tp'}, dimensions={0}, use_global_device_ids=true | all-gather | bytes 294912 | tf_op jit(solution)/shard_map/all_gather | solution.py:407
  566.5 52.3 %head_grad.4 = f32[768,2048]{1,0:T(8,128)} custom-call(s32[3]{0:T(128)} %get-tuple-element.67.meta, bf16[4,1024,1024]{2,1,0:T(8,128)(2,1)} %all-gather.45.cloned.1.call-done.ht, bf16[4,1024,768]{2,1,0:T(8,128)(2,1)} %bitcast.211, bf16[4,768,1024]{2,1,0:T(8,128)(2,1)} %bitcast.215, f32[4,1024,1]{2,1,0:T(8,128)} %copy.59.lt, f32[4,1024,1]{2,1,0:T(8,128)} %copy.60.ls, ...), custom_call_target="tpu_custom_call" | custom-call | flops 35433480192 | bytes 30408704 | tf_op jit(solution)/shard_map/head_grad/pallas_call | solution.py:182
  622.1 47.9 %head_grad.5 = f32[768,1536]{1,0:T(8,128)} custom-call(s32[3]{0:T(128)} %get-tuple-element.68.meta, bf16[4,1024,1024]{2,1,0:T(8,128)(2,1)} %all-gather.45.cloned.1.call-done.ht, bf16[4,1024,768]{2,1,0:T(8,128)(2,1)} %bitcast.212, bf16[4,768,1024]{2,1,0:T(8,128)(2,1)} %bitcast.216, f32[4,1024,1]{2,1,0:T(8,128)} %copy.61.lt, f32[4,1024,1]{2,1,0:T(8,128)} %copy.60.ls, ...), custom_call_target="tpu_custom_call" | custom-call | flops 26575110144 | bytes 22806528 | tf_op jit(solution)/shard_map/head_grad/pallas_call | solution.py:182
  671.0 105.2 %head_input_grad.1 = f32[1024,768]{1,0:T(8,128)} custom-call(s32[3]{0:T(128)} %get-tuple-element.69.meta, f32[1024,1]{1,0:T(8,128)} %copy.63.lt, f32[1024,1]{1,0:T(8,128)} %copy.64.ls, f32[1024,25600]{1,0:T(8,128)} %get-tuple-element.15.zt_own.zt, f32[1024,25600]{1,0:T(8,128)} %get-tuple-element.16.zs_own.zs, bf16[768,50304]{1,0:T(8,128)(2,1)} %ws.11), custom_call_target="tpu_custom_call" | custom-call | flops 80530636800 | bytes 249036800 | tf_op jit(solution)/shard_map/head_input_grad/pallas_call | solution.py:229
  792.7 15.1 %fusion.200 = f32[4096,1536]{1,0:T(8,128)} fusion(f32[768]{0:T(1024)S(1)} %copy-done.26, bf16[1,768,3072]{2,1,0:T(8,128)(2,1)} %param.17, s32[]{:T(128)S(6)} %select_n.29, bf16[4096,768]{1,0:T(8,128)(2,1)S(1)} %copy-done.2, f32[4096]{0:T(1024)S(1)} %add_rsqrt_fusion), kind=kOutput, calls=%fused_computation.197 | convolution fusion | flops 9676259328 | bytes 33836036 | tf_op jit(solution)/shard_map/sd,df->sf/dot_general | solution.py:41
  809.8 123.4 %head_grad.6.refs_2_ = f32[768,5632]{1,0:T(8,128)} custom-call(s32[3]{0:T(128)} %get-tuple-element.30.meta, bf16[4,1024,1024]{2,1,0:T(8,128)(2,1)} %all-gather.45.cloned.1.call-done.ht, bf16[4,1024,768]{2,1,0:T(8,128)(2,1)} %bitcast.213, bf16[4,768,1024]{2,1,0:T(8,128)(2,1)} %bitcast.217, f32[4,1024,1]{2,1,0:T(8,128)} %copy.65.lt, f32[4,1024,1]{2,1,0:T(8,128)} %copy.60.ls, ...), custom_call_target="tpu_custom_call" | custom-call | flops 97442070528 | bytes 83623936 | tf_op jit(solution)/shard_map/head_grad/pallas_call | solution.py:182
  935.2 8.6 fusion.117
  944.0 126.2 %head_grad.7.refs_3_ = f32[768,5632]{1,0:T(8,128)} custom-call(s32[3]{0:T(128)} %get-tuple-element.66.meta, bf16[4,1024,1024]{2,1,0:T(8,128)(2,1)} %all-gather.45.cloned.1.call-done.ht, bf16[4,1024,768]{2,1,0:T(8,128)(2,1)} %bitcast.214, bf16[4,768,1024]{2,1,0:T(8,128)(2,1)} %bitcast.218, f32[4,1024,1]{2,1,0:T(8,128)} %copy.67.lt, f32[4,1024,1]{2,1,0:T(8,128)} %copy.60.ls, ...), custom_call_target="tpu_custom_call" | custom-call | flops 97442070528 | bytes 83623936 | tf_op jit(solution)/shard_map/head_grad/pallas_call | solution.py:182
  1070.2 20.4 %fusion.8 = f32[1536,768]{1,0:T(8,128)} fusion(bf16[4096,768]{1,0:T(8,128)(2,1)} %all-gather.47.cloned.1.call-done, f32[4096,1536]{1,0:T(8,128)} %fusion.200), kind=kOutput, calls=%fused_computation.23 | convolution fusion | flops 9720299520 | bytes 36175872 | tf_op jit(solution)/shard_map/sf,sd->fd/dot_general | solution.py:41
  1091.7 32.5 %fusion.6 = bf16[4096,1536]{1,0:T(8,128)(2,1)} fusion(f32[4096,1536]{1,0:T(8,128)} %fusion.200, bf16[4096,768]{1,0:T(8,128)(2,1)} %all-gather.47.cloned.1.call-done, bf16[1,3072,768]{2,1,0:T(8,128)(2,1)} %param.18, s32[]{:T(128)S(6)} %select_n.29), kind=kOutput, calls=%fused_computation.9 | convolution fusion | flops 9789505536 | bytes 46399492 | tf_op jit(solution)/shard_map/sd,fd->sf/dot_general | solution.py:41
  1124.2 15.5 %fusion.199 = f32[768,1536]{1,0:T(8,128)} fusion(bf16[4096,1536]{1,0:T(8,128)(2,1)} %fusion.6, f32[768]{0:T(1024)S(1)} %copy-done.27, bf16[4096,768]{1,0:T(8,128)(2,1)S(1)} %bitcast.223, f32[4096]{0:T(1024)S(1)} %copy-done.20), kind=kOutput, calls=%fused_computation.196 | convolution fusion | flops 9676259328 | bytes 23612416 | tf_op jit(solution)/shard_map/sd,sf->df/dot_general | solution.py:41
  1139.7 10.5 convert_multiply_fusion
  1150.8 7.7 multiply_reduce_fusion
  1158.5 41.2 %all-reduce.1 = (f32[]{:T(128)}, f32[1,768]{1,0:T(1,128)}) all-reduce(f32[]{:T(128)} %get-tuple-element.51, f32[1,768]{1,0:T(1,128)S(1)} %broadcast_in_dim.10), channel_id=1, replica_groups=mesh['dp'=4,'tp'=2] {'dp','tp'}, use_global_device_ids=true, to_apply=%region_19.20 | all-reduce | flops 769 | bytes 6152 | tf_op jit(solution)/shard_map/psum | solution.py:477
  1200.5 99.1 %assemble.1 = f32[768,50304]{1,0:T(8,128)} custom-call(s32[3]{0:T(128)} %get-tuple-element.69.meta, f32[4,768,2048]{2,1,0:T(8,128)} %bitcast.221, f32[4,768,1536]{2,1,0:T(8,128)} %bitcast.225, f32[768,5632]{1,0:T(8,128)} %head_grad.6.refs_2_, f32[768,5632]{1,0:T(8,128)} %head_grad.7.refs_3_, f32[4,768,2048]{2,1,0:T(8,128)} %collective-permute-done.1.refs_4_, ...), custom_call_target="tpu_custom_call" | custom-call | flops 3863347200 | bytes 309067776 | tf_op jit(solution)/shard_map/assemble/pallas_call | solution.py:324
  1299.5 8.8 copy.90
  1308.3 4.8 copy.91
  (206 shorter events, 87.1 us)
Async XLA Ops:
  7.2 342.8 %copy-start = (bf16[1,768,1024]{2,1,0:T(8,128)(2,1)S(1)}, bf16[1,768,1024]{2,1,0:T(8,128)(2,1)}, u32[]{:S(2)}) copy-start(bf16[1,768,1024]{2,1,0:T(8,128)(2,1)} %param.20) | copy-start | bytes 4718596
  7.2 16.5 %all-gather.23.cloned.1.call-start = ((), (), s32[]{:S(2)}) async-start(), calls=%async_computation.9 | async-start | bytes 3145728 | tf_op jit(solution)/shard_map/all_gather | solution.py:395
  12.9 37.7 %reduce-scatter.9.cloned.1.call-start = ((), (), s32[]{:S(2)}) async-start(), calls=%async_computation.10 | async-start | bytes 6291456 | tf_op jit(solution)/shard_map/reduce_scatter | solution.py:398
  30.6 20.0 %copy-start.5 = (bf16[4,128,1024]{2,1,0:T(8,128)(2,1)S(1)}, bf16[4,128,1024]{2,1,0:T(8,128)(2,1)}, u32[]{:S(2)}) copy-start(bf16[4,128,1024]{2,1,0:T(8,128)(2,1)} %param.11) | copy-start | bytes 3145732
  40.1 24.1 %all-gather.25.cloned.1.call-start = ((), (), s32[]{:S(2)}) async-start(), calls=%async_computation.11 | async-start | bytes 3145728 | tf_op jit(solution)/shard_map/all_gather | solution.py:395
  54.8 34.9 %reduce-scatter.11.cloned.1.call-start = ((), (), s32[]{:S(2)}) async-start(), calls=%async_computation.12 | async-start | bytes 6291456 | tf_op jit(solution)/shard_map/reduce_scatter | solution.py:398
  79.2 23.4 %all-gather.27.cloned.1.call-start = ((), (), s32[]{:S(2)}) async-start(), calls=%async_computation.13 | async-start | bytes 3145728 | tf_op jit(solution)/shard_map/all_gather | solution.py:395
  93.3 34.9 %reduce-scatter.13.cloned.1.call-start = ((), (), s32[]{:S(2)}) async-start(), calls=%async_computation.14 | async-start | bytes 6291456 | tf_op jit(solution)/shard_map/reduce_scatter | solution.py:398
  117.6 24.1 %all-gather.29.cloned.1.call-start = ((), (), s32[]{:S(2)}) async-start(), calls=%async_computation.15 | async-start | bytes 3145728 | tf_op jit(solution)/shard_map/all_gather | solution.py:395
  132.4 34.9 %copy-start.8 = (bf16[4,128,1024]{2,1,0:T(8,128)(2,1)S(1)}, bf16[4,128,1024]{2,1,0:T(8,128)(2,1)}, u32[]{:S(2)}) copy-start(bf16[4,128,1024]{2,1,0:T(8,128)(2,1)} %copy-done.7) | copy-start | bytes 3145732
  132.4 34.8 %reduce-scatter.15.cloned.1.call-start = ((), (), s32[]{:S(2)}) async-start(), calls=%async_computation.16 | async-start | bytes 6291456 | tf_op jit(solution)/shard_map/reduce_scatter | solution.py:398
  156.7 24.1 %all-gather.31.cloned.1.call-start = ((), (), s32[]{:S(2)}) async-start(), calls=%async_computation.17 | async-start | bytes 3145728 | tf_op jit(solution)/shard_map/all_gather | solution.py:395
  171.5 34.8 %copy-start.10 = (bf16[4,128,1024]{2,1,0:T(8,128)(2,1)S(1)}, bf16[4,128,1024]{2,1,0:T(8,128)(2,1)}, u32[]{:S(2)}) copy-start(bf16[4,128,1024]{2,1,0:T(8,128)(2,1)} %copy-done.9) | copy-start | bytes 3145732
  171.5 34.8 %reduce-scatter.17.cloned.1.call-start = ((), (), s32[]{:S(2)}) async-start(), calls=%async_computation.18 | async-start | bytes 6291456 | tf_op jit(solution)/shard_map/reduce_scatter | solution.py:398
  195.8 24.1 %all-gather.33.cloned.1.call-start = ((), (), s32[]{:S(2)}) async-start(), calls=%async_computation.19 | async-start | bytes 3145728 | tf_op jit(solution)/shard_map/all_gather | solution.py:395
  210.6 34.9 %copy-start.12 = (bf16[4,128,1024]{2,1,0:T(8,128)(2,1)S(1)}, bf16[4,128,1024]{2,1,0:T(8,128)(2,1)}, u32[]{:S(2)}) copy-start(bf16[4,128,1024]{2,1,0:T(8,128)(2,1)} %copy-done.11) | copy-start | bytes 3145732
  210.6 34.8 %reduce-scatter.19.cloned.1.call-start = ((), (), s32[]{:S(2)}) async-start(), calls=%async_computation.20 | async-start | bytes 6291456 | tf_op jit(solution)/shard_map/reduce_scatter | solution.py:398
  234.9 24.1 %all-gather.35.cloned.1.call-start = ((), (), s32[]{:S(2)}) async-start(), calls=%async_computation.21 | async-start | bytes 3145728 | tf_op jit(solution)/shard_map/all_gather | solution.py:395
  249.7 34.9 %copy-start.14 = (bf16[4,128,1024]{2,1,0:T(8,128)(2,1)S(1)}, bf16[4,128,1024]{2,1,0:T(8,128)(2,1)}, u32[]{:S(2)}) copy-start(bf16[4,128,1024]{2,1,0:T(8,128)(2,1)} %copy-done.13) | copy-start | bytes 3145732
  249.7 34.9 %reduce-scatter.21.cloned.1.call-start = ((), (), s32[]{:S(2)}) async-start(), calls=%async_computation.22 | async-start | bytes 6291456 | tf_op jit(solution)/shard_map/reduce_scatter | solution.py:398
  274.0 13.5 %copy-start.23 = (f32[1,1024]{1,0:T(1,128)S(1)}, f32[1,1024]{1,0:T(1,128)}, u32[]{:S(2)}) copy-start(f32[1,1024]{1,0:T(1,128)} %get-tuple-element.58) | copy-start | bytes 12292
  274.0 24.1 %all-gather.37.cloned.1.call-start = ((), (), s32[]{:S(2)}) async-start(), calls=%async_computation.23 | async-start | bytes 3145728 | tf_op jit(solution)/shard_map/all_gather | solution.py:395
  288.8 24.4 %copy-start.28 = (f32[1,768]{1,0:T(1,128)S(1)}, f32[1,768]{1,0:T(1,128)}, u32[]{:S(2)}) copy-start(f32[1,768]{1,0:T(1,128)} %param.19) | copy-start | bytes 9220
  288.9 24.4 %copy-start.16 = (bf16[2,256,768]{2,1,0:T(8,128)(2,1)S(1)}, bf16[2,256,768]{2,1,0:T(8,128)(2,1)}, u32[]{:S(2)}) copy-start(bf16[2,256,768]{2,1,0:T(8,128)(2,1)} %param.12) | copy-start | bytes 2359300
  288.9 34.8 %reduce-scatter.23.cloned.1.call-start = ((), (), s32[]{:S(2)}) async-start(), calls=%async_computation.24 | async-start | bytes 6291456 | tf_op jit(solution)/shard_map/reduce_scatter | solution.py:398
  313.1 30.7 %all-gather.39.cloned.1.call-start = ((), (), s32[]{:S(2)}) async-start(), calls=%async_computation.25 | async-start | bytes 3145728 | tf_op jit(solution)/shard_map/all_gather | solution.py:402
  327.2 61.7 %all-gather.41.cloned.1.call-start = ((), (), s32[]{:S(2)}) async-start(), calls=%async_computation.26 | async-start | bytes 7077888 | tf_op jit(solution)/shard_map/all_gather | solution.py:378
  343.7 222.8 %all-gather.45.cloned.1.call-start = ((), (), s32[]{:S(2)}) async-start(), calls=%async_computation.28 | async-start | bytes 10485760 | tf_op jit(solution)/shard_map/all_gather | solution.py:403
  344.5 443.6 %all-gather.43.cloned.1.call-start = ((), (), s32[]{:S(2)}) async-start(), calls=%async_computation.27 | async-start | bytes 7077888 | tf_op jit(solution)/shard_map/all_gather | solution.py:367
  345.1 590.1 %all-gather.53.cloned.1.call-start = ((), (), s32[]{:S(2)}) async-start(), calls=%async_computation.32 | async-start | bytes 9437184 | tf_op jit(solution)/shard_map/all_gather | solution.py:449
  352.6 591.2 %all-gather.57.cloned.1.call-start = ((), (), s32[]{:S(2)}) async-start(), calls=%async_computation.34 | async-start | bytes 31457280 | tf_op jit(solution)/shard_map/all_gather | solution.py:434
  618.8 451.3 %all-gather.47.cloned.1.call-start = ((), (), s32[]{:S(2)}) async-start(), calls=%async_computation.29 | async-start | bytes 7077888 | tf_op jit(solution)/shard_map/all_gather | solution.py:448
  671.0 111.6 %copy-start.4 = (f32[512,768]{1,0:T(8,128)S(1)}, f32[512,768]{1,0:T(8,128)}, u32[]{:S(2)}) copy-start(f32[512,768]{1,0:T(8,128)} %copy-done.3) | copy-start | bytes 4718596
  671.0 111.6 %copy-start.22 = (f32[512]{0:T(512)S(1)}, f32[512]{0:T(512)}, u32[]{:S(2)}) copy-start(f32[512]{0:T(512)} %copy-done.21) | copy-start | bytes 6148
  778.8 3.8 collective-permute-start
  787.2 303.4 %all-gather.59.cloned.1.call-start = ((), (), s32[]{:S(2)}) async-start(), calls=%async_computation.35 | async-start | bytes 23592960 | tf_op jit(solution)/shard_map/all_gather | solution.py:434
  787.8 362.9 %all-gather.55.cloned.1.call-start = ((), (), s32[]{:S(2)}) async-start(), calls=%async_computation.33 | async-start | bytes 4718592 | tf_op jit(solution)/shard_map/all_gather | solution.py:476
  792.7 15.1 %copy-start.19 = (f32[4096]{0:T(1024)}, f32[4096]{0:T(1024)S(1)}, u32[]{:S(2)}) copy-start(f32[4096]{0:T(1024)S(1)} %add_rsqrt_fusion) | copy-start | bytes 49156
  943.8 256.6 %all-gather.51.cloned.1.call-start = ((), (), s32[]{:S(2)}) async-start(), calls=%async_computation.31 | async-start | bytes 14155776 | tf_op jit(solution)/shard_map/all_gather | solution.py:475
  943.9 256.6 %collective-permute-start.1 = (f32[4,768,2048]{2,1,0:T(8,128)}, f32[4,768,2048]{2,1,0:T(8,128)}, u32[]{:S(2)}, u32[]{:S(2)}) collective-permute-start(f32[4,768,2048]{2,1,0:T(8,128)} %bitcast.220), channel_id=1, source_target_pairs={{0,1},{1,0},{2,3},{3,2},{4,5},{5,4},{6,7},{7,6}} | collective-permute-start | bytes 75497480 | tf_op jit(solution)/shard_map/ppermute | solution.py:461
  1090.6 109.8 %all-gather.49.cloned.1.call-start = ((), (), s32[]{:S(2)}) async-start(), calls=%async_computation.30 | async-start | bytes 14155776 | tf_op jit(solution)/shard_map/all_gather | solution.py:474
  1090.7 33.5 %slice-start = ((s8[6291456]{0:T(1024)(128)(4,1)}), s8[4194304]{0:T(1024)(128)(4,1)S(1)}, s32[]{:S(2)}) async-start(s8[6291456]{0:T(1024)(128)(4,1)} %bitcast.222), calls=%async_computation.36 | async-start | bytes 8388608
  1090.7 33.5 %slice-start.1 = ((s8[6291456]{0:T(1024)(128)(4,1)}), s8[2097152]{0:T(1024)(128)(4,1)S(1)}, s32[]{:S(2)}) async-start(s8[6291456]{0:T(1024)(128)(4,1)} %bitcast.222), calls=%async_computation.37 | async-start | bytes 4194304
  1090.7 33.5 %copy-start.20 = (f32[4096]{0:T(1024)S(1)}, f32[4096]{0:T(1024)}, u32[]{:S(2)}) copy-start(f32[4096]{0:T(1024)} %copy-done.19) | copy-start | bytes 49156
  1090.7 33.5 %copy-start.27 = (f32[768]{0:T(1024)S(1)}, f32[768]{0:T(1024)}, u32[]{:S(2)}) copy-start(f32[768]{0:T(1024)} %copy-done.25) | copy-start | bytes 9220
  1090.7 109.7 %collective-permute-start.2 = (f32[4,768,1536]{2,1,0:T(8,128)}, f32[4,768,1536]{2,1,0:T(8,128)}, u32[]{:S(2)}, u32[]{:S(2)}) collective-permute-start(f32[4,768,1536]{2,1,0:T(8,128)} %bitcast.224), channel_id=1, source_target_pairs={{0,1},{1,0},{2,3},{3,2},{4,5},{5,4},{6,7},{7,6}} | collective-permute-start | bytes 56623112 | tf_op jit(solution)/shard_map/ppermute | solution.py:461
  1091.1 109.3 %collective-permute-start.4 = (f32[768,5632]{1,0:T(8,128)}, f32[768,5632]{1,0:T(8,128)}, u32[]{:S(2)}, u32[]{:S(2)}) collective-permute-start(f32[768,5632]{1,0:T(8,128)} %head_grad.7.refs_3_), channel_id=1, source_target_pairs={{0,1},{1,0},{2,3},{3,2},{4,5},{5,4},{6,7},{7,6}} | collective-permute-start | bytes 51904520 | tf_op jit(solution)/shard_map/ppermute | solution.py:461
  1091.2 109.2 %collective-permute-start.3 = (f32[768,5632]{1,0:T(8,128)}, f32[768,5632]{1,0:T(8,128)}, u32[]{:S(2)}, u32[]{:S(2)}) collective-permute-start(f32[768,5632]{1,0:T(8,128)} %head_grad.6.refs_2_), channel_id=1, source_target_pairs={{0,1},{1,0},{2,3},{3,2},{4,5},{5,4},{6,7},{7,6}} | collective-permute-start | bytes 51904520 | tf_op jit(solution)/shard_map/ppermute | solution.py:461
  (18 other events, 76.6 us)
Sparse Core Ops, SparseCore 0:
  13.1 10.5 all-gather.22
  40.2 10.3 reduce-scatter.8
  55.0 9.1 all-gather.24
  79.3 10.3 reduce-scatter.10
  93.4 9.1 all-gather.26
  117.8 10.3 reduce-scatter.12
  132.5 9.1 all-gather.28
  156.9 10.3 reduce-scatter.14
  171.7 9.0 all-gather.30
  196.0 10.3 reduce-scatter.16
  210.7 9.1 all-gather.32
  235.1 10.3 reduce-scatter.18
  249.8 9.1 all-gather.34
  274.2 10.3 reduce-scatter.20
  289.0 9.0 all-gather.36
  313.3 10.3 reduce-scatter.22
  327.4 9.1 all-gather.38
  343.9 41.1 all-gather.40
  386.8 81.9 all-gather.44
  470.5 39.8 all-gather.42
  512.2 49.6 all-gather.52
  619.0 221.9 all-gather.56
  842.8 39.8 all-gather.46
  884.3 170.2 all-gather.58
  1056.1 9.3 all-gather.54
  1090.7 26.2 all-gather.50
  1139.8 25.4 all-gather.48

commit v2 on v1

--- a/solution.py
+++ b/solution.py
@@ -11,6 +11,8 @@
 NORM_EPS = 1e-6
 NEG = -3.0e38
 BLK = 512
+PIECE = 64
+N_PIECE = BLK // PIECE
 N_BLK = 50
 N_OWN = 7
 N_SHARED = 4 * N_OWN
@@ -54,7 +56,25 @@
     return (cols >= 64 * core) & (cols < half_cols + 64 * core)
 
 
-def stats_kernel(half_cols, meta, ht, rs, wt, ws, zt_out, zs_out, st_out, mt, st, at, ms, ss):
+def join_rows(pieces, dst):
+    for j, piece in enumerate(pieces):
+        dst[j * PIECE:(j + 1) * PIECE, :] = piece[...]
+
+
+def piece_specs(first_blk, d_t, half_cols):
+    def spec(j):
+        def index(i, m):
+            return jnp.clip(N_PIECE * (first_blk(m) + i) + j - m[0], 0, half_cols // PIECE - 1), 0
+
+        return pl.BlockSpec((PIECE, d_t), index)
+
+    return [spec(j) for j in range(N_PIECE)]
+
+
+def stats_kernel(half_cols, meta, ht, rs, *refs):
+    pieces, refs = refs[:N_PIECE], refs[N_PIECE:]
+    ws, zt_out, zs_out, st_out, mt, st, at, ms, ss, wt = refs
+    join_rows(pieces, wt)
     blk = pl.program_id(0)
     valid = valid_cols(meta[0], blk, half_cols)
 
@@ -113,7 +133,7 @@
         in_specs=[
             pl.BlockSpec((rows, d_t), lambda k, m: (0, 0), pipeline_mode=pl.Buffered(1)),
             pl.BlockSpec((rows, d_s), lambda k, m: (0, 0), pipeline_mode=pl.Buffered(1)),
-            pl.BlockSpec((BLK, d_t), lambda k, m: (k, 0)),
+            *piece_specs(lambda m: 0, d_t, half_cols),
             pl.BlockSpec((d_s, BLK), lambda k, m: (0, k + (N_BLK - 1) * m[0])),
         ],
         out_specs=[
@@ -121,7 +141,7 @@
             pl.BlockSpec((rows, BLK), lambda k, m: (0, k)),
             pl.BlockSpec((rows, 128), lambda k, m: (0, 0)),
         ],
-        scratch_shapes=[pltpu.VMEM((rows, 128), jnp.float32)] * 5,
+        scratch_shapes=[pltpu.VMEM((rows, 128), jnp.float32)] * 5 + [pltpu.VMEM((BLK, d_t), jnp.bfloat16)],
     )
     return pl.pallas_call(
         functools.partial(stats_kernel, half_cols),
@@ -136,14 +156,16 @@
             flops=2 * rows * cols * (d_t + d_s), bytes_accessed=cols * (2 * (d_t + d_s) + 8 * rows),
             transcendentals=2 * rows * cols),
         name="head_stats",
-    )(meta, ht, rs, hts, head_s)
+    )(meta, ht, rs, *([hts] * N_PIECE), head_s)
 
 
 def logit_grad(zt, zs, lse_t, lse_s, coef):
     return (coef * (jnp.exp(zs - lse_s) - jnp.exp(zt - lse_t))).astype(jnp.bfloat16)
 
 
-def grad_kernel(half_cols, coef, meta, ht, rs, rst, lt, ls, wt, ws, zt_own, zs_own, out):
+def grad_kernel(half_cols, coef, meta, ht, rs, rst, lt, ls, *refs):
+    ws, zt_own, zs_own, out, wt = refs[N_PIECE:]
+    join_rows(refs[:N_PIECE], wt)
     own = meta[1]
     valid = valid_cols(meta[0], meta[2] + pl.program_id(0), half_cols)
     lg = logit_grad(zt_own[...], zs_own[...], lt[own], ls[own], coef)
@@ -171,12 +193,13 @@
             whole((groups, d_s, rows)),
             whole((groups, rows, 1)),
             whole((groups, rows, 1)),
-            pl.BlockSpec((BLK, d_t), lambda i, m: (m[2] + i, 0)),
+            *piece_specs(lambda m: m[2], d_t, half_cols),
             pl.BlockSpec((d_s, BLK), lambda i, m: (0, m[2] + i + (N_BLK - 1) * m[0])),
             pl.BlockSpec((rows, BLK), lambda i, m: (0, m[2] + i)),
             pl.BlockSpec((rows, BLK), lambda i, m: (0, m[2] + i)),
         ],
         out_specs=pl.BlockSpec((d_s, BLK), lambda i, m: (0, i)),
+        scratch_shapes=[pltpu.VMEM((BLK, d_t), jnp.bfloat16)],
     )
     cols = n_blocks * BLK
     return pl.pallas_call(
@@ -188,7 +211,7 @@
             flops=2 * rows * cols * (3 * d_t + 7 * d_s), bytes_accessed=cols * (2 * d_t + 6 * d_s + 8 * rows),
             transcendentals=8 * rows * cols),
         name="head_grad",
-    )(meta, ht_all, rs_all, rst_all, lse_t, lse_s, hts, head_s, zt, zs)
+    )(meta, ht_all, rs_all, rst_all, lse_t, lse_s, *([hts] * N_PIECE), head_s, zt, zs)
 
 
 def input_grad_kernel(coef, meta, lt, ls, zt, zs, ws, out):
@@ -340,6 +363,117 @@
     )(meta, *own, *partner)
 
 
+def teacher_kernel(n_layers, x, gain, w_up, w_down, h_out, ht_out, up_buf, down_buf, n_own, n_oth, act_own, act_oth,
+                   part_own, part_oth, part_in, w_sem, n_send, n_recv, p_send, p_recv):
+    core = lax.axis_index('tp')
+    other = {'tp': 1 - core}
+    mesh_id = pl.DeviceIdType.MESH
+    barrier = pltpu.get_barrier_semaphore()
+    pl.semaphore_signal(barrier, inc=1, device_id=other, device_id_type=mesh_id)
+    pl.semaphore_wait(barrier, 1)
+
+    def fetch(layer, slot):
+        return (pltpu.make_async_copy(w_up.at[layer], up_buf.at[slot], w_sem.at[0, slot]),
+                pltpu.make_async_copy(w_down.at[layer], down_buf.at[slot], w_sem.at[1, slot]))
+
+    def norm_exchange():
+        return pltpu.make_async_remote_copy(src_ref=n_own, dst_ref=n_oth, send_sem=n_send, recv_sem=n_recv,
+                                            device_id=other, device_id_type=mesh_id)
+
+    for copy in fetch(0, 0):
+        copy.start()
+    h_out[...] = x[...]
+    d_ff = up_buf.shape[2]
+    rows_all = x.shape[0]
+    half_rows = rows_all // 2
+
+    def up_proj(src, dst, slot):
+        for col in range(0, d_ff, 512):
+            pre = dot_f32(src[...], up_buf[slot, :, col:col + 512])
+            dst[:, col:col + 512] = gelu_tanh(pre).astype(jnp.bfloat16)
+
+    def layer_step(layer, carry):
+        slot = lax.rem(layer, 2)
+
+        @pl.when(layer + 1 < n_layers)
+        def _():
+            for copy in fetch(layer + 1, 1 - slot):
+                copy.start()
+
+        n_own[...] = (rms_parts(h_out[...])[0] * gain[pl.ds(layer, 1), :]).astype(jnp.bfloat16)
+        give = norm_exchange()
+        give.start()
+        up_copy, down_copy = fetch(layer, slot)
+        up_copy.wait()
+        up_proj(n_own, act_own, slot)
+        give.wait_recv()
+        up_proj(n_oth, act_oth, slot)
+        down_copy.wait()
+        sends = []
+        for half in range(2):
+            rows = pl.ds(half * half_rows, half_rows)
+            part_oth[rows, :] = dot_f32(act_oth[rows, :], down_buf[slot])
+            sends.append(pltpu.make_async_remote_copy(
+                src_ref=part_oth.at[rows, :], dst_ref=part_in.at[rows, :], send_sem=p_send.at[half],
+                recv_sem=p_recv.at[half], device_id=other, device_id_type=mesh_id))
+            sends[-1].start()
+        for half in range(2):
+            rows = pl.ds(half * half_rows, half_rows)
+            part_own[rows, :] = dot_f32(act_own[rows, :], down_buf[slot])
+        for half in range(2):
+            rows = pl.ds(half * half_rows, half_rows)
+            sends[half].wait_recv()
+            layer_out = (part_own[rows, :] + part_in[rows, :]).astype(jnp.bfloat16).astype(jnp.float32)
+            h_out[rows, :] = (h_out[rows, :].astype(jnp.float32) + layer_out).astype(jnp.bfloat16)
+        for half in range(2):
+            sends[half].wait_send()
+        give.wait_send()
+        return carry
+
+    lax.fori_loop(0, n_layers, layer_step, 0)
+    n_own[...] = rms_parts(h_out[...])[0].astype(jnp.bfloat16)
+    give = norm_exchange()
+    give.start()
+    ht_out[core] = n_own[...]
+    give.wait_recv()
+    ht_out[1 - core] = n_oth[...]
+    give.wait_send()
+
+
+def teacher(x, gain, w_up, w_down):
+    rows, d_t = x.shape
+    n_layers, _, d_ff = w_up.shape
+    vmem = pl.BlockSpec(memory_space=pltpu.VMEM)
+    any_spec = pl.BlockSpec(memory_space=pl.ANY)
+    return pl.pallas_call(
+        functools.partial(teacher_kernel, n_layers),
+        in_specs=[vmem, vmem, any_spec, any_spec],
+        out_specs=[vmem, vmem],
+        out_shape=[jax.ShapeDtypeStruct((rows, d_t), jnp.bfloat16),
+                   jax.ShapeDtypeStruct((2, rows, d_t), jnp.bfloat16)],
+        scratch_shapes=[
+            pltpu.VMEM((2, d_t, d_ff), jnp.bfloat16),
+            pltpu.VMEM((2, d_ff, d_t), jnp.bfloat16),
+            pltpu.VMEM((rows, d_t), jnp.bfloat16),
+            pltpu.VMEM((rows, d_t), jnp.bfloat16),
+            pltpu.VMEM((rows, d_ff), jnp.bfloat16),
+            pltpu.VMEM((rows, d_ff), jnp.bfloat16),
+            pltpu.VMEM((rows, d_t), jnp.float32),
+            pltpu.VMEM((rows, d_t), jnp.float32),
+            pltpu.VMEM((rows, d_t), jnp.float32),
+            pltpu.SemaphoreType.DMA((2, 2)),
+            pltpu.SemaphoreType.DMA,
+            pltpu.SemaphoreType.DMA,
+            pltpu.SemaphoreType.DMA((2,)),
+            pltpu.SemaphoreType.DMA((2,)),
+        ],
+        compiler_params=pltpu.CompilerParams(collective_id=0, has_side_effects=True, vmem_limit_bytes=VMEM_LIMIT),
+        cost_estimate=pl.CostEstimate(flops=8 * n_layers * rows * d_t * d_ff, bytes_accessed=4 * n_layers * d_t * d_ff,
+                                      transcendentals=2 * n_layers * rows * d_ff),
+        name="teacher",
+    )(x, gain, w_up, w_down)
+
+
 def after(value, *earlier):
     return lax.optimization_barrier((value, *earlier))[0]
 
@@ -380,8 +514,7 @@
         rst_all = jnp.swapaxes(rs_all, 1, 2)
         rs_grp = lax.dynamic_index_in_dim(rs_all, dp_idx, 0, keepdims=False)
 
-        padded = jnp.pad(head_t.T, ((64, N_BLK * BLK - half_cols), (0, 0)))
-        hts = lax.dynamic_slice_in_dim(padded, 64 - 64 * core, N_BLK * BLK, axis=0)
+        hts = head_t.T
 
         f_half = w_up.shape[1] // tp_size
         up_half = lax.dynamic_slice_in_dim(w_up, core * f_half, f_half, axis=1)
@@ -389,17 +522,10 @@
         pre_half = mat_mul('sd,df->sf', n_all, up_half)
         act_half = gelu_tanh(pre_half).astype(jnp.bfloat16)
 
-        hidden = x_teach
-        for layer_idx in range(w_up_t.shape[0]):
-            t_in = (rms_parts(hidden)[0] * gain_t[layer_idx]).astype(jnp.bfloat16)
-            gathered = lax.all_gather(t_in, 'tp', axis=1, tiled=True)
-            hidden_act = gelu_tanh(mat_mul('bsd,df->bsf', gathered, w_up_t[layer_idx])).astype(jnp.bfloat16)
-            partial_out = mat_mul('bsf,fd->bsd', hidden_act, w_down_t[layer_idx])
-            layer_out = lax.psum_scatter(partial_out, 'tp', scatter_dimension=1, tiled=True)
-            hidden = hidden + layer_out.astype(jnp.bfloat16)
-        feature = lax.all_to_all(hidden, 'tp', 0, 1, tiled=True)
-        final_norm = rms_parts(hidden)[0].astype(jnp.bfloat16)
-        ht_grp = lax.all_gather(final_norm, 'tp', axis=1, tiled=True).reshape(group_tok, d_t)
+        n_seq_t, half_seq, _ = x_teach.shape
+        hidden, ht_pair = teacher(x_teach.reshape(-1, d_t), gain_t, w_up_t, w_down_t)
+        feature = lax.all_to_all(hidden.reshape(n_seq_t, half_seq, d_t), 'tp', 0, 1, tiled=True)
+        ht_grp = jnp.swapaxes(ht_pair.reshape(tp_size, n_seq_t, half_seq, d_t), 0, 1).reshape(group_tok, d_t)
         ht_all = lax.all_gather(ht_grp, 'dp')
 
         meta0 = jnp.stack([core, dp_idx, jnp.int32(0)]).astype(jnp.int32)
@@ -474,7 +600,9 @@
         grad_up = lax.all_gather(up_part, 'tp', axis=1, tiled=True)[None]
         grad_down = lax.all_gather(down_part, 'tp', axis=0, tiled=True)[None]
         grad_proj = lax.all_gather(proj_part, 'tp', axis=1, tiled=True)[None]
-        grad_gain, err_sum = lax.psum((gain_part, err_total), both)
+        small = jnp.concatenate([gain_part, err_total[None], jnp.zeros((1023 - d_s,), jnp.float32)]).reshape(8, 128)
+        small = jnp.sum(lax.all_gather(small, both), axis=0).reshape(1024)
+        grad_gain, err_sum = small[:d_s], small[d_s]
         loss = feat_coef * err_sum + kl_coef * kl_total
         head_grad = assemble(meta0, own, partner, vocab)
         return loss, grad_up, grad_down, grad_gain[None], grad_proj, head_grad

time: 1330 us -> 1090 us (0.82)
  waiting for transfers between devices: 162 us -> 10.5 us
  matrix products: 241 us -> 118 us
  Pallas kernels: 700 us -> 812 us
  local copies, waits for them, and re-layouts: 86.7 us -> 50.5 us
  other arithmetic: 51.3 us -> 23.5 us
    dot_general x19 -> x10, matrix products: 241 us -> 118 us  [mat_mul(): jnp.einsum(subscripts, lhs_arr, rhs_arr, preferred_element_type=jnp.float32)]
    pallas_call x0 -> x1, Pallas kernels: none -> 104 us  [teacher(): pl.pallas_call(functools.partial(teacher_kernel, n_layers), in_specs=[vme...]
    reduce_scatter x8 -> x0, waiting for transfers between devices: 82.5 us -> none  [local_step(): lax.psum_scatter(partial_out, 'tp', scatter_dimension=1, tiled=True)]
    all_gather x9 -> x0, waiting for transfers between devices: 73.1 us -> none  [the longest x8 73.1 us: local_step(): gathered = lax.all_gather(t_in, 'tp', axis=1, tiled=True)]
    psum x1 -> x0, blocking collectives: 41.2 us -> none  [local_step(): grad_gain, err_sum = lax.psum((gain_part, err_total), both)]
    dynamic_slice x1 -> x0, local copies, waits for them, and re-layouts: 35 us -> none  [local_step(): hts = lax.dynamic_slice_in_dim(padded, 64 - 64 * core, N_BLK * BLK, axis=0)]
    all_gather x0 -> x1, blocking collectives: none -> 31.2 us  [local_step(): small = jnp.sum(lax.all_gather(small, both), axis=0).reshape(1024)]
    reduce_sum x11 -> x2, other arithmetic: 22.4 us -> 5.71 us  [rms_parts(): jnp.mean(vals32 * vals32, axis=-1, keepdims=True) + NORM_EPS]
  transfers between devices with their start and end apart: 32 -> 15, of which waited for: 17 -> 2; matrix products, arithmetic and copies ran while one was open for 15% -> 14% of each run, Pallas kernels for 45% -> 66%
where the time goes in v2:
time: 1090 us; the launch traced here: 1080 us
  Pallas kernels  812 us (74%)
  matrix products  118 us (11%)
  blocking collectives  50.6 us (5%)
  local copies, waits for them, and re-layouts  50.5 us (5%)
  other arithmetic  23.5 us (2%)
  between operations  17.2 us (2%)
    pallas_call x4, Pallas kernels, head_grad_blocks(): pl.pallas_call(functools.partial(grad_kernel, half_cols, coef), grid_spec...  350 us
    pallas_call x1, Pallas kernels, head_stats(): pl.pallas_call(functools.partial(stats_kernel, half_cols), grid_spec=grid...  154 us
    dot_general x10, matrix products, mat_mul(): jnp.einsum(subscripts, lhs_arr, rhs_arr, preferred_element_type=jnp.float32)  118 us
    pallas_call x1, Pallas kernels, head_input_grad(): pl.pallas_call(functools.partial(input_grad_kernel, coef), grid_spec=grid...  105 us
    pallas_call x1, Pallas kernels, teacher(): pl.pallas_call(functools.partial(teacher_kernel, n_layers), in_specs=[vme...  104 us
    pallas_call x1, Pallas kernels, assemble(): pl.pallas_call(functools.partial(assemble_kernel, len(own), n_buf), in_sp...  99.1 us
    all_gather x1, blocking collectives, local_step(): small = jnp.sum(lax.all_gather(small, both), axis=0).reshape(1024)  31.2 us
  transfers between devices with their start and end apart: 15, of which 2 were waited for; matrix products, arithmetic and copies ran while one was open for 14% of the time, Pallas kernels for 66%

profile of v2, /device:TPU:0, one launch (start us, length us, event | category | flops | bytes accessed | tf_op | source)
XLA Modules:
  0.0 1084.4 jit_solution(296821432575321135)
XLA Ops:
  7.2 1.5 fusion.35
  9.4 1.4 fusion.37
  10.8 7.6 fusion.16
  18.5 6.0 multiply_reduce_fusion.3
  24.5 1.1 copy-done.3
  25.6 1.0 multiply_convert_fusion.7
  26.9 104.3 %teacher.1 = (bf16[512,1024]{1,0:T(8,128)(2,1)}, bf16[2,512,1024]{2,1,0:T(8,128)(2,1)}) custom-call(bf16[512,1024]{1,0:T(8,128)(2,1)} %bitcast.191, f32[8,1024]{1,0:T(8,128)} %gain.1, bf16[8,1024,2048]{2,1,0:T(8,128)(2,1)} %w_up.1, bf16[8,2048,1024]{2,1,0:T(8,128)(2,1)} %w_down.1), custom_call_target="tpu_custom_call" | custom-call | flops 68719476736 | bytes 67108864 | tf_op jit(solution)/shard_map/teacher/pallas_call | solution.py:448
  131.3 3.1 copy.59
  136.8 8.8 copy.62
  145.6 2.8 dynamic-slice_bitcast_fusion.rs
  148.4 153.8 %head_stats.1 = (f32[1024,25600]{1,0:T(8,128)}, f32[1024,25600]{1,0:T(8,128)}, f32[1024,128]{1,0:T(8,128)}) custom-call(s32[3]{0:T(128)} %get-tuple-element.47.meta, bf16[1024,1024]{1,0:T(8,128)(2,1)} %bitcast.173, bf16[1024,768]{1,0:T(8,128)(2,1)} %dynamic-slice_bitcast_fusion.rs, bf16[25152,1024]{1,0:T(8,128)(2,1)} %bitcast.118, ...), custom_call_target="tpu_custom_call" | custom-call | flops 93952409600 | bytes 301465600 | tf_op jit(solution)/shard_map/head_stats/pallas_call | solution.py:146
  302.2 1.1 slice_bitcast_fusion
  303.4 14.6 %all-gather = f32[64,1024]{1,0:T(8,128)S(1)} all-gather(f32[8,1024]{1,0:T(8,128)S(1)} %copy.60), channel_id=2, replica_groups=mesh['dp'=4,'tp'=2] {'dp','tp'}, dimensions={0}, use_global_device_ids=true | all-gather | bytes 294912 | tf_op jit(solution)/shard_map/all_gather | solution.py:533
  319.0 2.0 copy.63.lt
  321.0 2.0 copy.64.ls
  323.0 52.9 %head_grad.4 = f32[768,2048]{1,0:T(8,128)} custom-call(s32[3]{0:T(128)} %get-tuple-element.45.meta, bf16[4,1024,1024]{2,1,0:T(8,128)(2,1)} %all-gather.16.cloned.1.call-done.ht, bf16[4,1024,768]{2,1,0:T(8,128)(2,1)} %bitcast.160, bf16[4,768,1024]{2,1,0:T(8,128)(2,1)} %bitcast.164, f32[4,1024,1]{2,1,0:T(8,128)} %copy.63.lt, f32[4,1024,1]{2,1,0:T(8,128)} %copy.64.ls, ...), custom_call_target="tpu_custom_call" | custom-call | flops 35433480192 | bytes 30408704 | tf_op jit(solution)/shard_map/head_grad/pallas_call | solution.py:205
  376.1 1.1 copy-done.8
  377.2 4.7 all_to_all.4
  382.2 2.7 multiply_convert_fusion.5
  384.9 0.7 dynamic-slice_bitcast_fusion.1
  385.6 1.0 copy.68.ls
  386.7 2.0 copy.65.lt
  388.7 44.4 %head_grad.5 = f32[768,1536]{1,0:T(8,128)} custom-call(s32[3]{0:T(128)} %get-tuple-element.46.meta, bf16[4,1024,1024]{2,1,0:T(8,128)(2,1)} %all-gather.16.cloned.1.call-done.ht, bf16[4,1024,768]{2,1,0:T(8,128)(2,1)} %bitcast.161, bf16[4,768,1024]{2,1,0:T(8,128)(2,1)} %bitcast.165, f32[4,1024,1]{2,1,0:T(8,128)} %copy.65.lt, f32[4,1024,1]{2,1,0:T(8,128)} %copy.64.ls, ...), custom_call_target="tpu_custom_call" | custom-call | flops 26575110144 | bytes 22806528 | tf_op jit(solution)/shard_map/head_grad/pallas_call | solution.py:205
  433.1 1.1 copy.67.lt
  434.2 105.1 %head_input_grad.1 = f32[1024,768]{1,0:T(8,128)} custom-call(s32[3]{0:T(128)} %get-tuple-element.47.meta, f32[1024,1]{1,0:T(8,128)} %copy.67.lt, f32[1024,1]{1,0:T(8,128)} %copy.68.ls, f32[1024,25600]{1,0:T(8,128)} %get-tuple-element.19.refs_9_.zt, f32[1024,25600]{1,0:T(8,128)} %get-tuple-element.20.refs_10_.zs, bf16[768,50304]{1,0:T(8,128)(2,1)} %refs_8_.9), custom_call_target="tpu_custom_call" | custom-call | flops 80530636800 | bytes 249036800 | tf_op jit(solution)/shard_map/head_input_grad/pallas_call | solution.py:252
  539.3 2.6 constant_dynamic-slice_fusion
  542.1 3.5 collective-permute-done
  545.7 3.4 multiply_reduce_fusion.2
  549.1 1.2 multiply_convert_fusion.6
  551.4 4.2 fusion.7
  556.0 14.9 %fusion.28 = f32[4096,1536]{1,0:T(8,128)} fusion(f32[768]{0:T(1024)S(1)} %copy-done.19, bf16[1,768,3072]{2,1,0:T(8,128)(2,1)} %param.17, s32[]{:T(128)S(6)} %select_n.25, bf16[4096,768]{1,0:T(8,128)(2,1)S(1)} %copy-done.2, f32[4096]{0:T(1024)S(1)} %add_rsqrt_fusion), kind=kOutput, calls=%fused_computation.34 | convolution fusion | flops 9676259328 | bytes 33836036 | tf_op jit(solution)/shard_map/sd,df->sf/dot_general | solution.py:43
  570.9 2.0 copy.69.lt
  572.9 125.2 %head_grad.6.refs_2_ = f32[768,5632]{1,0:T(8,128)} custom-call(s32[3]{0:T(128)} %get-tuple-element.32.meta, bf16[4,1024,1024]{2,1,0:T(8,128)(2,1)} %all-gather.16.cloned.1.call-done.ht, bf16[4,1024,768]{2,1,0:T(8,128)(2,1)} %bitcast.162, bf16[4,768,1024]{2,1,0:T(8,128)(2,1)} %bitcast.166, f32[4,1024,1]{2,1,0:T(8,128)} %copy.69.lt, f32[4,1024,1]{2,1,0:T(8,128)} %copy.64.ls, ...), custom_call_target="tpu_custom_call" | custom-call | flops 97442070528 | bytes 83623936 | tf_op jit(solution)/shard_map/head_grad/pallas_call | solution.py:205
  698.1 2.0 copy.71.lt
  700.3 127.2 %head_grad.7.refs_3_ = f32[768,5632]{1,0:T(8,128)} custom-call(s32[3]{0:T(128)} %get-tuple-element.44.meta, bf16[4,1024,1024]{2,1,0:T(8,128)(2,1)} %all-gather.16.cloned.1.call-done.ht, bf16[4,1024,768]{2,1,0:T(8,128)(2,1)} %bitcast.163, bf16[4,768,1024]{2,1,0:T(8,128)(2,1)} %bitcast.167, f32[4,1024,1]{2,1,0:T(8,128)} %copy.71.lt, f32[4,1024,1]{2,1,0:T(8,128)} %copy.64.ls, ...), custom_call_target="tpu_custom_call" | custom-call | flops 97442070528 | bytes 83623936 | tf_op jit(solution)/shard_map/head_grad/pallas_call | solution.py:205
  827.5 8.6 fusion.21
  836.1 20.7 %fusion.8 = f32[1536,768]{1,0:T(8,128)} fusion(bf16[4096,768]{1,0:T(8,128)(2,1)} %all-gather.18.cloned.1.call-done, f32[4096,1536]{1,0:T(8,128)} %fusion.28), kind=kOutput, calls=%fused_computation.14 | convolution fusion | flops 9720299520 | bytes 36175872 | tf_op jit(solution)/shard_map/sf,sd->fd/dot_general | solution.py:43
  856.9 5.3 all-gather.32.cloned.1.call-done
  862.8 30.9 %fusion.6 = bf16[4096,1536]{1,0:T(8,128)(2,1)} fusion(f32[4096,1536]{1,0:T(8,128)} %fusion.28, bf16[4096,768]{1,0:T(8,128)(2,1)} %all-gather.18.cloned.1.call-done, bf16[1,3072,768]{2,1,0:T(8,128)(2,1)} %param.18, s32[]{:T(128)S(6)} %select_n.25), kind=kOutput, calls=%fused_computation.8 | convolution fusion | flops 9789505536 | bytes 46399492 | tf_op jit(solution)/shard_map/sd,fd->sf/dot_general | solution.py:43
  893.8 15.4 %fusion.27 = f32[768,1536]{1,0:T(8,128)} fusion(bf16[4096,1536]{1,0:T(8,128)(2,1)} %fusion.6, f32[768]{0:T(1024)S(1)} %copy-done.20, bf16[4096,768]{1,0:T(8,128)(2,1)S(1)} %bitcast.171, f32[4096]{0:T(1024)S(1)} %copy-done.15), kind=kOutput, calls=%fused_computation.33 | convolution fusion | flops 9676259328 | bytes 23612416 | tf_op jit(solution)/shard_map/sd,sf->df/dot_general | solution.py:43
  909.8 10.5 convert_multiply_fusion
  920.3 7.7 multiply_reduce_fusion
  928.0 0.7 maximum_bitcast_fusion
  928.7 31.2 %all_gather.51 = f32[8,8,128]{2,1,0:T(8,128)S(1)} all-gather(f32[1,8,128]{2,1,0:T(8,128)S(1)} %maximum_bitcast_fusion), channel_id=1, replica_groups=mesh['dp'=4,'tp'=2] {'dp','tp'}, dimensions={0}, use_global_device_ids=true | all-gather | bytes 36864 | tf_op jit(solution)/shard_map/all_gather | solution.py:604
  961.9 99.1 %assemble.1 = f32[768,50304]{1,0:T(8,128)} custom-call(s32[3]{0:T(128)} %get-tuple-element.47.meta, f32[4,768,2048]{2,1,0:T(8,128)} %bitcast.169, f32[4,768,1536]{2,1,0:T(8,128)} %bitcast.175, f32[768,5632]{1,0:T(8,128)} %head_grad.6.refs_2_, f32[768,5632]{1,0:T(8,128)} %head_grad.7.refs_3_, f32[4,768,2048]{2,1,0:T(8,128)} %collective-permute-done.1.refs_4_, ...), custom_call_target="tpu_custom_call" | custom-call | flops 3863347200 | bytes 309067776 | tf_op jit(solution)/shard_map/assemble/pallas_call | solution.py:347
  1061.0 8.8 copy.98
  1069.8 4.8 copy.99
  1074.5 1.7 copy.100
  (108 shorter events, 8.7 us)
Async XLA Ops:
  7.2 375.0 %copy-start = (bf16[1,768,1024]{2,1,0:T(8,128)(2,1)S(1)}, bf16[1,768,1024]{2,1,0:T(8,128)(2,1)}, u32[]{:S(2)}) copy-start(bf16[1,768,1024]{2,1,0:T(8,128)(2,1)} %param.20) | copy-start | bytes 4718596
  7.2 129.6 %all-gather.14.cloned.1.call-start = ((), (), s32[]{:S(2)}) async-start(), calls=%async_computation.1 | async-start | bytes 7077888 | tf_op jit(solution)/shard_map/all_gather | solution.py:512
  9.4 1.4 copy-start.18
  10.8 7.6 copy-start.5
  24.4 1.2 copy-start.3
  24.5 1.2 copy-start.16
  26.7 296.4 %all-gather.16.cloned.1.call-start = ((), (), s32[]{:S(2)}) async-start(), calls=%async_computation.2 | async-start | bytes 10485760 | tf_op jit(solution)/shard_map/all_gather | solution.py:529
  134.4 417.0 %all-gather.20.cloned.1.call-start = ((), (), s32[]{:S(2)}) async-start(), calls=%async_computation.4 | async-start | bytes 7077888 | tf_op jit(solution)/shard_map/all_gather | solution.py:501
  135.1 565.0 %all-gather.30.cloned.1.call-start = ((), (), s32[]{:S(2)}) async-start(), calls=%async_computation.9 | async-start | bytes 31457280 | tf_op jit(solution)/shard_map/all_gather | solution.py:560
  319.0 4.0 copy-start.9
  319.0 4.0 copy-start.13
  376.0 1.2 copy-start.8
  376.0 6.2 copy-start.7
  376.0 451.4 %all-gather.26.cloned.1.call-start = ((), (), s32[]{:S(2)}) async-start(), calls=%async_computation.7 | async-start | bytes 9437184 | tf_op jit(solution)/shard_map/all_gather | solution.py:575
  377.2 9.5 copy-start.10
  384.9 451.3 %all-gather.18.cloned.1.call-start = ((), (), s32[]{:S(2)}) async-start(), calls=%async_computation.3 | async-start | bytes 7077888 | tf_op jit(solution)/shard_map/all_gather | solution.py:574
  388.7 44.4 %copy-start.11 = (f32[4,1024,1]{1,0,2:T(4,128)S(1)}, f32[4,1024,1]{1,0,2:T(4,128)}, u32[]{:S(2)}) copy-start(f32[4,1024,1]{1,0,2:T(4,128)} %copy-done.9) | copy-start | bytes 49156
  434.2 111.5 %copy-start.4 = (f32[512,768]{1,0:T(8,128)S(1)}, f32[512,768]{1,0:T(8,128)}, u32[]{:S(2)}) copy-start(f32[512,768]{1,0:T(8,128)} %copy-done.3) | copy-start | bytes 4718596
  434.2 111.5 %copy-start.17 = (f32[512]{0:T(512)S(1)}, f32[512]{0:T(512)}, u32[]{:S(2)}) copy-start(f32[512]{0:T(512)} %copy-done.16) | copy-start | bytes 6148
  541.9 3.8 collective-permute-start
  550.3 5.3 copy-start.19
  550.3 311.9 %all-gather.32.cloned.1.call-start = ((), (), s32[]{:S(2)}) async-start(), calls=%async_computation.10 | async-start | bytes 23592960 | tf_op jit(solution)/shard_map/all_gather | solution.py:560
  551.1 369.2 %all-gather.28.cloned.1.call-start = ((), (), s32[]{:S(2)}) async-start(), calls=%async_computation.8 | async-start | bytes 4718592 | tf_op jit(solution)/shard_map/all_gather | solution.py:602
  551.4 4.6 copy-start.2
  556.0 14.9 %copy-start.14 = (f32[4096]{0:T(1024)}, f32[4096]{0:T(1024)S(1)}, u32[]{:S(2)}) copy-start(f32[4096]{0:T(1024)S(1)} %add_rsqrt_fusion) | copy-start | bytes 49156
  572.9 125.2 %copy-start.12 = (f32[4,1024,1]{1,0,2:T(4,128)S(1)}, f32[4,1024,1]{1,0,2:T(4,128)}, u32[]{:S(2)}) copy-start(f32[4,1024,1]{1,0,2:T(4,128)} %copy-done.9) | copy-start | bytes 49156
  700.1 261.8 %collective-permute-start.1 = (f32[4,768,2048]{2,1,0:T(8,128)}, f32[4,768,2048]{2,1,0:T(8,128)}, u32[]{:S(2)}, u32[]{:S(2)}) collective-permute-start(f32[4,768,2048]{2,1,0:T(8,128)} %bitcast.168), channel_id=1, source_target_pairs={{0,1},{1,0},{2,3},{3,2},{4,5},{5,4},{6,7},{7,6}} | collective-permute-start | bytes 75497480 | tf_op jit(solution)/shard_map/ppermute | solution.py:587
  836.1 125.7 %all-gather.24.cloned.1.call-start = ((), (), s32[]{:S(2)}) async-start(), calls=%async_computation.6 | async-start | bytes 14155776 | tf_op jit(solution)/shard_map/all_gather | solution.py:601
  856.8 105.0 %all-gather.22.cloned.1.call-start = ((), (), s32[]{:S(2)}) async-start(), calls=%async_computation.5 | async-start | bytes 14155776 | tf_op jit(solution)/shard_map/all_gather | solution.py:600
  862.2 31.5 %slice-start = ((s8[6291456]{0:T(1024)(128)(4,1)}), s8[4194304]{0:T(1024)(128)(4,1)S(1)}, s32[]{:S(2)}) async-start(s8[6291456]{0:T(1024)(128)(4,1)} %bitcast.170), calls=%async_computation.11 | async-start | bytes 8388608
  862.2 31.5 %slice-start.1 = ((s8[6291456]{0:T(1024)(128)(4,1)}), s8[2097152]{0:T(1024)(128)(4,1)S(1)}, s32[]{:S(2)}) async-start(s8[6291456]{0:T(1024)(128)(4,1)} %bitcast.170), calls=%async_computation.12 | async-start | bytes 4194304
  862.2 31.5 %copy-start.15 = (f32[4096]{0:T(1024)S(1)}, f32[4096]{0:T(1024)}, u32[]{:S(2)}) copy-start(f32[4096]{0:T(1024)} %copy-done.14) | copy-start | bytes 49156
  862.2 31.5 %copy-start.20 = (f32[768]{0:T(1024)S(1)}, f32[768]{0:T(1024)}, u32[]{:S(2)}) copy-start(f32[768]{0:T(1024)} %copy-done.18) | copy-start | bytes 9220
  862.2 99.6 %collective-permute-start.2 = (f32[4,768,1536]{2,1,0:T(8,128)}, f32[4,768,1536]{2,1,0:T(8,128)}, u32[]{:S(2)}, u32[]{:S(2)}) collective-permute-start(f32[4,768,1536]{2,1,0:T(8,128)} %bitcast.174), channel_id=1, source_target_pairs={{0,1},{1,0},{2,3},{3,2},{4,5},{5,4},{6,7},{7,6}} | collective-permute-start | bytes 56623112 | tf_op jit(solution)/shard_map/ppermute | solution.py:587
  862.3 99.6 %collective-permute-start.4 = (f32[768,5632]{1,0:T(8,128)}, f32[768,5632]{1,0:T(8,128)}, u32[]{:S(2)}, u32[]{:S(2)}) collective-permute-start(f32[768,5632]{1,0:T(8,128)} %head_grad.7.refs_3_), channel_id=1, source_target_pairs={{0,1},{1,0},{2,3},{3,2},{4,5},{5,4},{6,7},{7,6}} | collective-permute-start | bytes 51904520 | tf_op jit(solution)/shard_map/ppermute | solution.py:587
  862.8 99.1 %collective-permute-start.3 = (f32[768,5632]{1,0:T(8,128)}, f32[768,5632]{1,0:T(8,128)}, u32[]{:S(2)}, u32[]{:S(2)}) collective-permute-start(f32[768,5632]{1,0:T(8,128)} %head_grad.6.refs_2_), channel_id=1, source_target_pairs={{0,1},{1,0},{2,3},{3,2},{4,5},{5,4},{6,7},{7,6}} | collective-permute-start | bytes 51904520 | tf_op jit(solution)/shard_map/ppermute | solution.py:587
  1060.9 8.8 slice-start.2
  1060.9 8.8 slice-start.3
  1061.0 8.8 slice-start.4
  1069.7 4.8 copy-start.6
  1069.7 6.5 copy-start.1
Sparse Core Ops, SparseCore 0:
  26.8 43.0 all-gather.13
  134.5 84.6 all-gather.15
  221.0 39.8 all-gather.19
  376.1 222.0 all-gather.29
  599.9 48.6 all-gather.25
  650.3 39.8 all-gather.17
  691.9 170.2 all-gather.31
  864.3 11.2 all-gather.27
  877.8 26.7 all-gather.23
  909.3 26.1 all-gather.21

commit v3 on v2

--- a/solution.py
+++ b/solution.py
@@ -17,7 +17,7 @@
 N_OWN = 7
 N_SHARED = 4 * N_OWN
 OWN_SPLIT = (4, 3)
-RED_SPLIT = (11, 11)
+RED_SPLIT = (7, 7, 8)
 VMEM_LIMIT = 60 * 1024 * 1024
 
 
@@ -163,21 +163,112 @@
     return (coef * (jnp.exp(zs - lse_s) - jnp.exp(zt - lse_t))).astype(jnp.bfloat16)
 
 
-def grad_kernel(half_cols, coef, meta, ht, rs, rst, lt, ls, *refs):
-    ws, zt_own, zs_own, out, wt = refs[N_PIECE:]
+def grad_kernel(half_cols, coef, hook, meta, ht, rs, rst, lt, ls, *refs):
+    ws, zt_own, zs_own = refs[N_PIECE:N_PIECE + 3]
+    extra, refs = refs[N_PIECE + 3:len(refs) - hook.n_tail], refs[:N_PIECE] + refs[len(refs) - hook.n_tail:]
+    out, wt = hook.bind(meta, extra, refs[N_PIECE:])
+    hook(0)
     join_rows(refs[:N_PIECE], wt)
     own = meta[1]
     valid = valid_cols(meta[0], meta[2] + pl.program_id(0), half_cols)
     lg = logit_grad(zt_own[...], zs_own[...], lt[own], ls[own], coef)
     out[...] = dot_f32(rst[own], lg)
+    hook(1)
     for other in range(1, 4):
         grp = lax.rem(own + other, 4)
         zt = jnp.where(valid, dot_rows(ht[grp], wt[...]), NEG)
         zs = jnp.where(valid, dot_f32(rs[grp], ws[...]), NEG)
         out[...] += dot_f32(rst[grp], logit_grad(zt, zs, lt[grp], ls[grp], coef))
-
-
-def head_grad_blocks(n_blocks, meta, ht_all, rs_all, rst_all, lse_t, lse_s, hts, head_s, zt, zs, half_cols, coef):
+        hook(1 + other)
+
+
+class NoCopies:
+    n_tail = 2
+
+    def bind(self, meta, extra, tail):
+        return tail
+
+    def __call__(self, point):
+        pass
+
+
+class BlockCopies:
+    n_tail = 6
+
+    def __init__(self, n_arr, jobs, n_steps, batch):
+        self.n_arr, self.jobs, self.n_steps, self.batch = n_arr, jobs, n_steps, batch
+
+    def bind(self, meta, extra, tail):
+        self.core = meta[0]
+        self.own, self.partner = extra[:self.n_arr], extra[self.n_arr:]
+        out, self.full, wt, self.bufs, self.in_sem, self.out_sem = tail
+        return out, wt
+
+    def start_in(self, slot, job):
+        kind, half, k = job
+        piece, dst, sem = block_pieces()[k], self.bufs.at[slot], self.in_sem.at[slot]
+        if kind == 'own':
+            pltpu.make_async_copy(piece_view(self.own, piece, 0, BLK), dst, sem).start()
+            return
+
+        @pl.when(self.core == half)
+        def _():
+            pltpu.make_async_copy(piece_view(self.own, piece, 0, BLK), dst, sem).start()
+
+        @pl.when(self.core != half)
+        def _():
+            pltpu.make_async_copy(piece_view(self.partner, piece, 0, BLK), dst, sem).start()
+
+    def out_copy(self, slot, job):
+        _, half, k = job
+        half = self.core if half is None else half
+        col = pl.multiple_of((N_BLK - 1) * BLK * half + k * BLK, 128)
+        return pltpu.make_async_copy(self.bufs.at[slot], self.full.at[:, pl.ds(col, BLK)], self.out_sem.at[slot])
+
+    def __call__(self, point):
+        for step in range(self.n_steps):
+            first = 2 * step * self.batch
+            batches = (self.jobs[first:first + self.batch], self.jobs[first + self.batch:first + 2 * self.batch])
+
+            @pl.when(pl.program_id(0) == step)
+            def _(batches=batches):
+                if point in (2, 4):
+                    for slot, job in enumerate(batches[point // 2 - 1]):
+                        self.out_copy(slot, job).wait()
+                if point in (0, 2):
+                    for slot, job in enumerate(batches[point // 2]):
+                        self.start_in(slot, job)
+                if point in (1, 3):
+                    for slot, job in enumerate(batches[point // 2]):
+                        pltpu.make_async_copy(self.bufs.at[slot], self.bufs.at[slot], self.in_sem.at[slot]).wait()
+                        self.out_copy(slot, job).start()
+
+
+EARLY_PARTS = (0, len(OWN_SPLIT))
+EARLY_OWN_PART = len(OWN_SPLIT) + 1
+
+
+def early_jobs():
+    pieces = block_pieces()
+    both = [('pair', half, k) for k in range(N_BLK) for half in range(2)
+            if pieces[k][0] in EARLY_PARTS and (half, k) != (1, 0)]
+    return both + [('own', None, k) for k in range(N_BLK) if pieces[k][0] == EARLY_OWN_PART]
+
+
+def head_grad_blocks(n_blocks, meta, ht_all, rs_all, rst_all, lse_t, lse_s, hts, head_s, zt, zs, half_cols, coef,
+                     own=None, partner=None):
+    hook, extra = NoCopies(), ()
+    out_specs = [pl.BlockSpec((head_s.shape[0], BLK), lambda i, m: (0, i))]
+    out_shape = [jax.ShapeDtypeStruct((head_s.shape[0], n_blocks * BLK), jnp.float32)]
+    scratch = [pltpu.VMEM((BLK, ht_all.shape[2]), jnp.bfloat16)]
+    if own is not None:
+        batch = 4
+        extra = (*own, *partner)
+        hook = BlockCopies(len(own), early_jobs(), n_blocks, batch)
+        out_specs.append(pl.BlockSpec(memory_space=pl.ANY))
+        out_shape.append(jax.ShapeDtypeStruct(head_s.shape, jnp.float32))
+        scratch += [pltpu.VMEM((batch, head_s.shape[0], BLK), jnp.float32),
+                    pltpu.SemaphoreType.DMA((batch,)), pltpu.SemaphoreType.DMA((batch,))]
     groups, rows, d_t = ht_all.shape
     d_s = rs_all.shape[2]
 
@@ -197,21 +288,21 @@
             pl.BlockSpec((d_s, BLK), lambda i, m: (0, m[2] + i + (N_BLK - 1) * m[0])),
             pl.BlockSpec((rows, BLK), lambda i, m: (0, m[2] + i)),
             pl.BlockSpec((rows, BLK), lambda i, m: (0, m[2] + i)),
-        ],
-        out_specs=pl.BlockSpec((d_s, BLK), lambda i, m: (0, i)),
-        scratch_shapes=[pltpu.VMEM((BLK, d_t), jnp.bfloat16)],
+        ] + [pl.BlockSpec(memory_space=pl.ANY)] * len(extra),
+        out_specs=out_specs,
+        scratch_shapes=scratch,
     )
     cols = n_blocks * BLK
     return pl.pallas_call(
-        functools.partial(grad_kernel, half_cols, coef),
+        functools.partial(grad_kernel, half_cols, coef, hook),
         grid_spec=grid_spec,
-        out_shape=jax.ShapeDtypeStruct((d_s, cols), jnp.float32),
+        out_shape=out_shape,
         compiler_params=pltpu.CompilerParams(dimension_semantics=("arbitrary",), vmem_limit_bytes=VMEM_LIMIT),
         cost_estimate=pl.CostEstimate(
             flops=2 * rows * cols * (3 * d_t + 7 * d_s), bytes_accessed=cols * (2 * d_t + 6 * d_s + 8 * rows),
             transcendentals=8 * rows * cols),
         name="head_grad",
-    )(meta, ht_all, rs_all, rst_all, lse_t, lse_s, *([hts] * N_PIECE), head_s, zt, zs)
+    )(meta, ht_all, rs_all, rst_all, lse_t, lse_s, *([hts] * N_PIECE), head_s, zt, zs, *extra)
 
 
 def input_grad_kernel(coef, meta, lt, ls, zt, zs, ws, out):
@@ -224,8 +315,11 @@
 
     @pl.when(blk < last)
     def _():
-        lg = logit_grad(zt[...], zs[...], lt[...], ls[...], coef)
-        out[...] += dot_rows(lg, ws[...])
+        step = 256
+        for row in range(0, out.shape[0], step):
+            rows = pl.ds(row, step)
+            lg = logit_grad(zt[rows, :], zs[rows, :], lt[rows, :], ls[rows, :], coef)
+            out[rows, :] += dot_rows(lg, ws[...])
 
     @pl.when(blk == last)
     def _():
@@ -287,16 +381,22 @@
 
 def assemble_kernel(n_arr, n_buf, meta, *refs):
     own, partner = refs[:n_arr], refs[n_arr:2 * n_arr]
-    out, bufs, seam_a, seam_b, in_sem, out_sem, seam_sem = refs[2 * n_arr:]
+    out, bufs, seam_a, seam_b, in_sem, out_sem, seam_sem = refs[2 * n_arr + 1:]
     core = meta[0]
     pieces = block_pieces()
     seam_col = (N_BLK - 1) * BLK
-    jobs = [(0, pieces[k], 0, k * BLK, BLK) for k in range(N_BLK - 1)]
+    late = [k for k in range(1, N_BLK - 1) if pieces[k][0] not in EARLY_PARTS + (EARLY_OWN_PART,)]
+    jobs = [(half, pieces[k], 0, seam_col * half + k * BLK, BLK) for k in late for half in range(2)]
+    jobs += [(None, pieces[k], 0, pl.multiple_of(seam_col * (1 - core) + k * BLK, 128), BLK)
+             for k in range(N_BLK) if pieces[k][0] == EARLY_OWN_PART]
     jobs.append((1, pieces[0], 128, seam_col + 128, BLK - 128))
-    jobs += [(1, pieces[k], 0, seam_col + k * BLK, BLK) for k in range(1, N_BLK - 1)]
     jobs.append((1, pieces[N_BLK - 1], 0, seam_col + (N_BLK - 1) * BLK, 128))
 
     def fetch(half, piece, extra, width, dst, sem):
+        if half is None:
+            pltpu.make_async_copy(piece_view(partner, piece, extra, width), dst, sem).start()
+            return
+
         @pl.when(core == half)
         def _():
             pltpu.make_async_copy(piece_view(own, piece, extra, width), dst, sem).start()
@@ -340,13 +440,13 @@
     seam.wait()
 
 
-def assemble(meta, own, partner, vocab):
+def assemble(meta, own, partner, full, vocab):
     d_s = own[0].shape[-2]
     n_buf = 8
     any_spec = pl.BlockSpec(memory_space=pl.ANY)
     return pl.pallas_call(
         functools.partial(assemble_kernel, len(own), n_buf),
-        in_specs=[pl.BlockSpec(memory_space=pltpu.SMEM)] + [any_spec] * (2 * len(own)),
+        in_specs=[pl.BlockSpec(memory_space=pltpu.SMEM)] + [any_spec] * (2 * len(own) + 1),
         out_specs=any_spec,
         out_shape=jax.ShapeDtypeStruct((d_s, vocab), jnp.float32),
         scratch_shapes=[
@@ -357,10 +457,11 @@
             pltpu.SemaphoreType.DMA((n_buf,)),
             pltpu.SemaphoreType.DMA((2,)),
         ],
+        input_output_aliases={2 * len(own) + 1: 0},
         compiler_params=pltpu.CompilerParams(vmem_limit_bytes=VMEM_LIMIT),
         cost_estimate=pl.CostEstimate(flops=d_s * vocab * 100, bytes_accessed=8 * d_s * vocab, transcendentals=0),
         name="assemble",
-    )(meta, *own, *partner)
+    )(meta, *own, *partner, full)
 
 
 def teacher_kernel(n_layers, x, gain, w_up, w_down, h_out, ht_out, up_buf, down_buf, n_own, n_oth, act_own, act_oth,
@@ -544,15 +645,15 @@
         lse_t = lse_t[..., None]
         lse_s = lse_s[..., None]
 
-        def blocks(base, count, lse):
+        def blocks(base, count, lse, *arrays):
             meta = jnp.stack([core, dp_idx, base]).astype(jnp.int32)
             return head_grad_blocks(count, meta, ht_all, rs_all, rst_all, lse, lse_s, hts, head_s, zt, zs,
-                                    half_cols, kl_coef)
+                                    half_cols, kl_coef, *arrays)
 
         own_parts = []
         base, lse_o = dp_idx * N_OWN, lse_t
         for count in OWN_SPLIT:
-            own_parts.append(blocks(base, count, lse_o))
+            own_parts.append(blocks(base, count, lse_o)[0])
             base = base + count
             lse_o = after(lse_t, own_parts[-1])
         shared = []
@@ -575,18 +676,26 @@
         err_all = lax.all_gather(err_grad, both, axis=0, tiled=True)
 
         lse_r = after(lse_t, full_in_grad)
-        redundant = []
+        own, partner = [], []
+
+        def exchange(part):
+            partner.append(lax.ppermute(part, 'tp', swap))
+            own.append(part)
+
+        for part in shared:
+            exchange(part)
         base = jnp.int32(N_SHARED)
-        for count in RED_SPLIT:
-            redundant.append(blocks(base, count, lse_r))
+        full = None
+        for part_idx, count in enumerate(RED_SPLIT):
+            last = part_idx == len(RED_SPLIT) - 1
+            arrays = ([own[0], own[0], own[2], own[3]], [partner[0], partner[0], partner[2], own[3]]) if last else ()
+            part, *rest = blocks(base, count, lse_r, *arrays)
+            full = rest[0] if rest else None
+            exchange(part)
             base = base + count
-            lse_r = after(lse_t, redundant[-1])
-        own = shared + redundant
-        partner = []
-        for part in own:
-            partner.append(lax.ppermute(part, 'tp', swap))
-
-        resid_all = after(resid_all, redundant[-1])
+            lse_r = after(lse_t, part)
+
+        resid_all = after(resid_all, own[-1])
         act_grad = mat_mul('sd,fd->sf', resid_all, down_half)
         pre_grad = gelu_back(pre_half, act_grad).astype(jnp.bfloat16)
         up_part = mat_mul('sd,sf->df', n_all, pre_grad)
@@ -604,7 +713,7 @@
         small = jnp.sum(lax.all_gather(small, both), axis=0).reshape(1024)
         grad_gain, err_sum = small[:d_s], small[d_s]
         loss = feat_coef * err_sum + kl_coef * kl_total
-        head_grad = assemble(meta0, own, partner, vocab)
+        head_grad = assemble(meta0, own, partner, full, vocab)
         return loss, grad_up, grad_down, grad_gain[None], grad_proj, head_grad
 
     in_specs = (P('dp', 'tp', None), P(('dp', 'tp'), None, None), P(None, None, 'tp'), P(None, 'tp', None),

time: 1090 us -> 1120 us (1.028)
  waiting for transfers between devices: 10.5 us -> 54.2 us
  blocking collectives: 50.6 us -> 30.8 us
    pallas_call x4 -> x5, Pallas kernels: 350 us -> 401 us  [head_grad_blocks(): pl.pallas_call(functools.partial(grad_kernel, half_cols, coef, hook), gri...]
    pallas_call x1, Pallas kernels: 99.1 us -> 48.2 us  [assemble(): pl.pallas_call(functools.partial(assemble_kernel, len(own), n_buf), in_sp...]
    all_gather x2, waiting for transfers between devices: 5.34 us -> 49.2 us  [local_step(): shared.append(lax.all_gather(part, 'dp'))]
    all_gather x1, blocking collectives: 31.2 us -> 12.1 us  [local_step(): small = jnp.sum(lax.all_gather(small, both), axis=0).reshape(1024)]
  transfers between devices with their start and end apart: 15 -> 16, of which waited for: 2 -> 2; matrix products, arithmetic and copies ran while one was open for 14% -> 14% of each run, Pallas kernels for 66% -> 64%
where the time goes in v3:
time: 1120 us; the launch traced here: 1110 us
  Pallas kernels  810 us (72%)
  matrix products  119 us (11%)
  waiting for transfers between devices  54.2 us (5%)
  local copies, waits for them, and re-layouts  52.2 us (5%)
  blocking collectives  30.8 us (3%)
  other arithmetic  23.7 us (2%)
  between operations  17.6 us (2%)
    pallas_call x5, Pallas kernels, head_grad_blocks(): pl.pallas_call(functools.partial(grad_kernel, half_cols, coef, hook), gri...  401 us
    pallas_call x1, Pallas kernels, head_stats(): pl.pallas_call(functools.partial(stats_kernel, half_cols), grid_spec=grid...  154 us
    dot_general x10, matrix products, mat_mul(): jnp.einsum(subscripts, lhs_arr, rhs_arr, preferred_element_type=jnp.float32)  119 us
    pallas_call x1, Pallas kernels, teacher(): pl.pallas_call(functools.partial(teacher_kernel, n_layers), in_specs=[vme...  104 us
    pallas_call x1, Pallas kernels, head_input_grad(): pl.pallas_call(functools.partial(input_grad_kernel, coef), grid_spec=grid...  103 us
    all_gather x2, waiting for transfers between devices, local_step(): shared.append(lax.all_gather(part, 'dp'))  49.2 us
    pallas_call x1, Pallas kernels, assemble(): pl.pallas_call(functools.partial(assemble_kernel, len(own), n_buf), in_sp...  48.2 us
  transfers between devices with their start and end apart: 16, of which 2 were waited for; matrix products, arithmetic and copies ran while one was open for 14% of the time, Pallas kernels for 64%

profile of v3, /device:TPU:0, one launch (start us, length us, event | category | flops | bytes accessed | tf_op | source)
XLA Modules:
  0.0 1110.1 jit_solution(6851289636263426584)
XLA Ops:
  7.2 1.5 fusion.35
  9.4 1.4 fusion.37
  10.8 7.6 fusion.16
  18.5 6.0 multiply_reduce_fusion.3
  24.5 1.2 copy-done.3
  25.6 1.1 multiply_convert_fusion.7
  27.0 104.3 %teacher.1 = (bf16[512,1024]{1,0:T(8,128)(2,1)}, bf16[2,512,1024]{2,1,0:T(8,128)(2,1)}) custom-call(bf16[512,1024]{1,0:T(8,128)(2,1)} %bitcast.203, f32[8,1024]{1,0:T(8,128)} %gain.1, bf16[8,1024,2048]{2,1,0:T(8,128)(2,1)} %w_up.1, bf16[8,2048,1024]{2,1,0:T(8,128)(2,1)} %w_down.1), custom_call_target="tpu_custom_call" | custom-call | flops 68719476736 | bytes 67108864 | tf_op jit(solution)/shard_map/teacher/pallas_call | solution.py:549
  131.4 3.1 copy.65
  136.3 8.8 copy.68
  145.1 3.0 dynamic-slice_bitcast_fusion.rs
  148.1 153.7 %head_stats.1 = (f32[1024,25600]{1,0:T(8,128)}, f32[1024,25600]{1,0:T(8,128)}, f32[1024,128]{1,0:T(8,128)}) custom-call(s32[3]{0:T(128)} %get-tuple-element.54.meta, bf16[1024,1024]{1,0:T(8,128)(2,1)} %bitcast.185, bf16[1024,768]{1,0:T(8,128)(2,1)} %dynamic-slice_bitcast_fusion.rs, bf16[25152,1024]{1,0:T(8,128)(2,1)} %bitcast.118, ...), custom_call_target="tpu_custom_call" | custom-call | flops 93952409600 | bytes 301465600 | tf_op jit(solution)/shard_map/head_stats/pallas_call | solution.py:146
  301.8 1.1 slice_bitcast_fusion
  303.1 14.0 %all-gather = f32[64,1024]{1,0:T(8,128)S(1)} all-gather(f32[8,1024]{1,0:T(8,128)S(1)} %copy.66), channel_id=2, replica_groups=mesh['dp'=4,'tp'=2] {'dp','tp'}, dimensions={0}, use_global_device_ids=true | all-gather | bytes 294912 | tf_op jit(solution)/shard_map/all_gather | solution.py:634
  318.2 2.0 copy.69.lt
  320.2 1.9 copy.70.ls
  322.1 52.9 %head_grad.5 = f32[768,2048]{1,0:T(8,128)} custom-call(s32[3]{0:T(128)} %get-tuple-element.52.meta, bf16[4,1024,1024]{2,1,0:T(8,128)(2,1)} %all-gather.16.cloned.1.call-done.ht, bf16[4,1024,768]{2,1,0:T(8,128)(2,1)} %bitcast.168, bf16[4,768,1024]{2,1,0:T(8,128)(2,1)} %bitcast.173, f32[4,1024,1]{2,1,0:T(8,128)} %copy.69.lt, f32[4,1024,1]{2,1,0:T(8,128)} %copy.70.ls, ...), custom_call_target="tpu_custom_call" | custom-call | flops 35433480192 | bytes 30408704 | tf_op jit(solution)/shard_map/head_grad/pallas_call | solution.py:296
  376.3 4.7 all_to_all.4
  381.2 2.5 multiply_convert_fusion.5
  383.9 0.7 dynamic-slice_bitcast_fusion.1
  384.6 1.0 copy.74.ls
  385.6 2.0 copy.71.lt
  387.6 44.4 %head_grad.6 = f32[768,1536]{1,0:T(8,128)} custom-call(s32[3]{0:T(128)} %get-tuple-element.53.meta, bf16[4,1024,1024]{2,1,0:T(8,128)(2,1)} %all-gather.16.cloned.1.call-done.ht, bf16[4,1024,768]{2,1,0:T(8,128)(2,1)} %bitcast.169, bf16[4,768,1024]{2,1,0:T(8,128)(2,1)} %bitcast.174, f32[4,1024,1]{2,1,0:T(8,128)} %copy.71.lt, f32[4,1024,1]{2,1,0:T(8,128)} %copy.70.ls, ...), custom_call_target="tpu_custom_call" | custom-call | flops 26575110144 | bytes 22806528 | tf_op jit(solution)/shard_map/head_grad/pallas_call | solution.py:296
  432.1 1.0 copy.73.lt
  433.1 103.0 %head_input_grad.1 = f32[1024,768]{1,0:T(8,128)} custom-call(s32[3]{0:T(128)} %get-tuple-element.54.meta, f32[1024,1]{1,0:T(8,128)} %copy.73.lt, f32[1024,1]{1,0:T(8,128)} %copy.74.ls, f32[1024,25600]{1,0:T(8,128)} %get-tuple-element.22.refs_9_.zt, f32[1024,25600]{1,0:T(8,128)} %get-tuple-element.23.refs_10_.zs, bf16[768,50304]{1,0:T(8,128)(2,1)} %refs_8_.11), custom_call_target="tpu_custom_call" | custom-call | flops 80530636800 | bytes 249036800 | tf_op jit(solution)/shard_map/head_input_grad/pallas_call | solution.py:346
  536.1 2.7 constant_dynamic-slice_fusion
  538.8 3.7 collective-permute-done
  542.5 3.4 multiply_reduce_fusion.2
  545.9 1.2 multiply_convert_fusion.6
  548.1 49.1 %all-gather.30.cloned.1.call-done = f32[3072,2048]{1,0:T(8,128)} async-done(((f32[768,2048]{1,0:T(8,128)}), f32[3072,2048]{1,0:T(8,128)}) %all-gather.30.cloned.1.call-update) | async-done | bytes 25165840 | tf_op jit(solution)/shard_map/all_gather | solution.py:661
  597.3 2.0 copy.75.lt
  599.3 84.7 %head_grad.7.refs_13_.refs_2_ = f32[768,3584]{1,0:T(8,128)} custom-call(s32[3]{0:T(128)} %get-tuple-element.38.meta, bf16[4,1024,1024]{2,1,0:T(8,128)(2,1)} %all-gather.16.cloned.1.call-done.ht, bf16[4,1024,768]{2,1,0:T(8,128)(2,1)} %bitcast.170, bf16[4,768,1024]{2,1,0:T(8,128)(2,1)} %bitcast.175, f32[4,1024,1]{2,1,0:T(8,128)} %copy.75.lt, ...), custom_call_target="tpu_custom_call" | custom-call | flops 62008590336 | bytes 53215232 | tf_op jit(solution)/shard_map/head_grad/pallas_call | solution.py:296
  684.5 4.3 fusion.7
  689.3 15.0 %fusion.28 = f32[4096,1536]{1,0:T(8,128)} fusion(f32[768]{0:T(1024)S(1)} %copy-done.20, bf16[1,768,3072]{2,1,0:T(8,128)(2,1)} %param.17, s32[]{:T(128)S(6)} %select_n.25, bf16[4096,768]{1,0:T(8,128)(2,1)S(1)} %copy-done.2, f32[4096]{0:T(1024)S(1)} %add_rsqrt_fusion), kind=kOutput, calls=%fused_computation.34 | convolution fusion | flops 9676259328 | bytes 33836036 | tf_op jit(solution)/shard_map/sd,df->sf/dot_general | solution.py:43
  704.3 2.0 copy.77.lt
  706.2 85.5 %head_grad.8.refs_14_.refs_18_.refs_3_ = f32[768,3584]{1,0:T(8,128)} custom-call(s32[3]{0:T(128)} %get-tuple-element.50.meta, bf16[4,1024,1024]{2,1,0:T(8,128)(2,1)} %all-gather.16.cloned.1.call-done.ht, bf16[4,1024,768]{2,1,0:T(8,128)(2,1)} %bitcast.171, bf16[4,768,1024]{2,1,0:T(8,128)(2,1)} %bitcast.176, f32[4,1024,1]{2,1,0:T(8,128)} %copy.77.lt, ...), custom_call_target="tpu_custom_call" | custom-call | flops 62008590336 | bytes 53215232 | tf_op jit(solution)/shard_map/head_grad/pallas_call | solution.py:296
  791.7 2.0 copy.79.lt
  793.7 8.6 fusion.21
  802.4 133.2 %head_grad.9 = (f32[768,4096]{1,0:T(8,128)}, f32[768,50304]{1,0:T(8,128)}) custom-call(s32[3]{0:T(128)} %get-tuple-element.51.meta, bf16[4,1024,1024]{2,1,0:T(8,128)(2,1)} %all-gather.16.cloned.1.call-done.ht, bf16[4,1024,768]{2,1,0:T(8,128)(2,1)} %bitcast.172, bf16[4,768,1024]{2,1,0:T(8,128)(2,1)} %bitcast.177, f32[4,1024,1]{2,1,0:T(8,128)} %copy.79.lt, ...), custom_call_target="tpu_custom_call" | custom-call | flops 70866960384 | bytes 60817408 | tf_op jit(solution)/shard_map/head_grad/pallas_call | solution.py:296
  935.6 20.4 %fusion.8 = f32[1536,768]{1,0:T(8,128)} fusion(bf16[4096,768]{1,0:T(8,128)(2,1)} %all-gather.18.cloned.1.call-done, f32[4096,1536]{1,0:T(8,128)} %fusion.28), kind=kOutput, calls=%fused_computation.14 | convolution fusion | flops 9720299520 | bytes 36175872 | tf_op jit(solution)/shard_map/sf,sd->fd/dot_general | solution.py:43
  956.8 32.3 %fusion.6 = bf16[4096,1536]{1,0:T(8,128)(2,1)} fusion(f32[4096,1536]{1,0:T(8,128)} %fusion.28, bf16[4096,768]{1,0:T(8,128)(2,1)} %all-gather.18.cloned.1.call-done, bf16[1,3072,768]{2,1,0:T(8,128)(2,1)} %param.18, s32[]{:T(128)S(6)} %select_n.25), kind=kOutput, calls=%fused_computation.8 | convolution fusion | flops 9789505536 | bytes 46399492 | tf_op jit(solution)/shard_map/sd,fd->sf/dot_general | solution.py:43
  989.2 15.5 %fusion.27 = f32[768,1536]{1,0:T(8,128)} fusion(bf16[4096,1536]{1,0:T(8,128)(2,1)} %fusion.6, f32[768]{0:T(1024)S(1)} %copy-done.21, bf16[4096,768]{1,0:T(8,128)(2,1)S(1)} %bitcast.183, f32[4096]{0:T(1024)S(1)} %copy-done.16), kind=kOutput, calls=%fused_computation.33 | convolution fusion | flops 9676259328 | bytes 23612416 | tf_op jit(solution)/shard_map/sd,sf->df/dot_general | solution.py:43
  1005.3 10.4 convert_multiply_fusion
  1015.7 7.7 multiply_reduce_fusion
  1024.2 12.1 %all_gather.53 = f32[8,8,128]{2,1,0:T(8,128)S(1)} all-gather(f32[1,8,128]{2,1,0:T(8,128)S(1)} %maximum_bitcast_fusion), channel_id=1, replica_groups=mesh['dp'=4,'tp'=2] {'dp','tp'}, dimensions={0}, use_global_device_ids=true | all-gather | bytes 36864 | tf_op jit(solution)/shard_map/all_gather | solution.py:713
  1038.1 48.2 %assemble.1 = f32[768,50304]{1,0:T(8,128)} custom-call(s32[3]{0:T(128)} %get-tuple-element.54.meta, f32[4,768,2048]{2,1,0:T(8,128)} %bitcast.181, f32[4,768,1536]{2,1,0:T(8,128)} %bitcast.187, f32[768,3584]{1,0:T(8,128)} %head_grad.7.refs_13_.refs_2_, f32[768,3584]{1,0:T(8,128)} %head_grad.8.refs_14_.refs_18_.refs_3_, ...), custom_call_target="tpu_custom_call", output_to_operand_aliasing={{}: (11, {})} | custom-call | flops 3863347200 | bytes 309067776 | tf_op jit(solution)/shard_map/assemble/pallas_call | solution.py:447
  1086.4 8.8 copy.107
  1095.2 4.8 copy.108
  1100.0 1.7 copy.109
  (114 shorter events, 10.5 us)
Async XLA Ops:
  7.2 374.1 %copy-start = (bf16[1,768,1024]{2,1,0:T(8,128)(2,1)S(1)}, bf16[1,768,1024]{2,1,0:T(8,128)(2,1)}, u32[]{:S(2)}) copy-start(bf16[1,768,1024]{2,1,0:T(8,128)(2,1)} %param.20) | copy-start | bytes 4718596
  7.2 129.1 %all-gather.14.cloned.1.call-start = ((), (), s32[]{:S(2)}) async-start(), calls=%async_computation.1 | async-start | bytes 7077888 | tf_op jit(solution)/shard_map/all_gather | solution.py:613
  9.4 1.4 copy-start.19
  10.8 7.7 copy-start.5
  24.5 1.2 copy-start.3
  24.5 1.2 copy-start.17
  26.8 295.3 %all-gather.16.cloned.1.call-start = ((), (), s32[]{:S(2)}) async-start(), calls=%async_computation.2 | async-start | bytes 10485760 | tf_op jit(solution)/shard_map/all_gather | solution.py:630
  134.5 462.8 %all-gather.30.cloned.1.call-start = ((), (), s32[]{:S(2)}) async-start(), calls=%async_computation.9 | async-start | bytes 31457280 | tf_op jit(solution)/shard_map/all_gather | solution.py:661
  318.2 3.9 copy-start.9
  318.2 3.9 copy-start.14
  375.0 1.2 copy-start.8
  375.1 6.2 copy-start.7
  375.1 309.4 %all-gather.20.cloned.1.call-start = ((), (), s32[]{:S(2)}) async-start(), calls=%async_computation.4 | async-start | bytes 7077888 | tf_op jit(solution)/shard_map/all_gather | solution.py:602
  375.7 418.0 %all-gather.26.cloned.1.call-start = ((), (), s32[]{:S(2)}) async-start(), calls=%async_computation.7 | async-start | bytes 9437184 | tf_op jit(solution)/shard_map/all_gather | solution.py:676
  376.3 9.4 copy-start.10
  383.8 551.8 %all-gather.18.cloned.1.call-start = ((), (), s32[]{:S(2)}) async-start(), calls=%async_computation.3 | async-start | bytes 7077888 | tf_op jit(solution)/shard_map/all_gather | solution.py:675
  387.6 44.5 %copy-start.11 = (f32[4,1024,1]{1,0,2:T(4,128)S(1)}, f32[4,1024,1]{1,0,2:T(4,128)}, u32[]{:S(2)}) copy-start(f32[4,1024,1]{1,0,2:T(4,128)} %copy-done.9) | copy-start | bytes 49156
  433.1 109.4 %copy-start.4 = (f32[512,768]{1,0:T(8,128)S(1)}, f32[512,768]{1,0:T(8,128)}, u32[]{:S(2)}) copy-start(f32[512,768]{1,0:T(8,128)} %copy-done.3) | copy-start | bytes 4718596
  433.1 109.4 %copy-start.18 = (f32[512]{0:T(512)S(1)}, f32[512]{0:T(512)}, u32[]{:S(2)}) copy-start(f32[512]{0:T(512)} %copy-done.17) | copy-start | bytes 6148
  538.7 3.8 collective-permute-start
  547.1 409.1 %all-gather.32.cloned.1.call-start = ((), (), s32[]{:S(2)}) async-start(), calls=%async_computation.10 | async-start | bytes 23592960 | tf_op jit(solution)/shard_map/all_gather | solution.py:661
  547.9 467.8 %all-gather.28.cloned.1.call-start = ((), (), s32[]{:S(2)}) async-start(), calls=%async_computation.8 | async-start | bytes 4718592 | tf_op jit(solution)/shard_map/all_gather | solution.py:711
  597.3 205.1 %collective-permute-start.1 = (f32[4,768,2048]{2,1,0:T(8,128)}, f32[4,768,2048]{2,1,0:T(8,128)}, u32[]{:S(2)}, u32[]{:S(2)}) collective-permute-start(f32[4,768,2048]{2,1,0:T(8,128)} %bitcast.178), channel_id=1, source_target_pairs={{0,1},{1,0},{2,3},{3,2},{4,5},{5,4},{6,7},{7,6}} | collective-permute-start | bytes 75497480 | tf_op jit(solution)/shard_map/ppermute | solution.py:682
  684.0 4.8 copy-start.20
  684.0 118.4 %collective-permute-start.2 = (f32[768,3584]{1,0:T(8,128)}, f32[768,3584]{1,0:T(8,128)}, u32[]{:S(2)}, u32[]{:S(2)}) collective-permute-start(f32[768,3584]{1,0:T(8,128)} %head_grad.7.refs_13_.refs_2_), channel_id=1, source_target_pairs={{0,1},{1,0},{2,3},{3,2},{4,5},{5,4},{6,7},{7,6}} | collective-permute-start | bytes 33030152 | tf_op jit(solution)/shard_map/ppermute | solution.py:682
  684.5 4.8 copy-start.2
  689.3 15.0 %copy-start.15 = (f32[4096]{0:T(1024)}, f32[4096]{0:T(1024)S(1)}, u32[]{:S(2)}) copy-start(f32[4096]{0:T(1024)S(1)} %add_rsqrt_fusion) | copy-start | bytes 49156
  689.3 15.0 %copy-start.12 = (f32[4,1024,1]{1,0,2:T(4,128)S(1)}, f32[4,1024,1]{1,0,2:T(4,128)}, u32[]{:S(2)}) copy-start(f32[4,1024,1]{1,0,2:T(4,128)} %copy-done.9) | copy-start | bytes 49156
  706.2 85.5 %copy-start.13 = (f32[4,1024,1]{1,0,2:T(4,128)S(1)}, f32[4,1024,1]{1,0,2:T(4,128)}, u32[]{:S(2)}) copy-start(f32[4,1024,1]{1,0,2:T(4,128)} %copy-done.9) | copy-start | bytes 49156
  802.3 235.8 %all-gather.24.cloned.1.call-start = ((), (), s32[]{:S(2)}) async-start(), calls=%async_computation.6 | async-start | bytes 14155776 | tf_op jit(solution)/shard_map/all_gather | solution.py:710
  956.1 82.0 %all-gather.22.cloned.1.call-start = ((), (), s32[]{:S(2)}) async-start(), calls=%async_computation.5 | async-start | bytes 14155776 | tf_op jit(solution)/shard_map/all_gather | solution.py:709
  956.2 33.0 %slice-start = ((s8[6291456]{0:T(1024)(128)(4,1)}), s8[4194304]{0:T(1024)(128)(4,1)S(1)}, s32[]{:S(2)}) async-start(s8[6291456]{0:T(1024)(128)(4,1)} %bitcast.182), calls=%async_computation.11 | async-start | bytes 8388608
  956.2 33.0 %slice-start.1 = ((s8[6291456]{0:T(1024)(128)(4,1)}), s8[2097152]{0:T(1024)(128)(4,1)S(1)}, s32[]{:S(2)}) async-start(s8[6291456]{0:T(1024)(128)(4,1)} %bitcast.182), calls=%async_computation.12 | async-start | bytes 4194304
  956.2 33.0 %copy-start.16 = (f32[4096]{0:T(1024)S(1)}, f32[4096]{0:T(1024)}, u32[]{:S(2)}) copy-start(f32[4096]{0:T(1024)} %copy-done.15) | copy-start | bytes 49156
  956.2 33.0 %copy-start.21 = (f32[768]{0:T(1024)S(1)}, f32[768]{0:T(1024)}, u32[]{:S(2)}) copy-start(f32[768]{0:T(1024)} %copy-done.19) | copy-start | bytes 9220
  956.2 81.9 %collective-permute-start.3 = (f32[4,768,1536]{2,1,0:T(8,128)}, f32[4,768,1536]{2,1,0:T(8,128)}, u32[]{:S(2)}, u32[]{:S(2)}) collective-permute-start(f32[4,768,1536]{2,1,0:T(8,128)} %bitcast.186), channel_id=1, source_target_pairs={{0,1},{1,0},{2,3},{3,2},{4,5},{5,4},{6,7},{7,6}} | collective-permute-start | bytes 56623112 | tf_op jit(solution)/shard_map/ppermute | solution.py:682
  956.3 81.8 %collective-permute-start.4 = (f32[768,3584]{1,0:T(8,128)}, f32[768,3584]{1,0:T(8,128)}, u32[]{:S(2)}, u32[]{:S(2)}) collective-permute-start(f32[768,3584]{1,0:T(8,128)} %head_grad.8.refs_14_.refs_18_.refs_3_), channel_id=1, source_target_pairs={{0,1},{1,0},{2,3},{3,2},{4,5},{5,4},{6,7},{7,6}} | collective-permute-start | bytes 33030152 | tf_op jit(solution)/shard_map/ppermute | solution.py:682
  956.8 81.4 %collective-permute-start.5 = (f32[768,4096]{1,0:T(8,128)}, f32[768,4096]{1,0:T(8,128)}, u32[]{:S(2)}, u32[]{:S(2)}) collective-permute-start(f32[768,4096]{1,0:T(8,128)} %get-tuple-element.29.refs_4_), channel_id=1, source_target_pairs={{0,1},{1,0},{2,3},{3,2},{4,5},{5,4},{6,7},{7,6}} | collective-permute-start | bytes 37748744 | tf_op jit(solution)/shard_map/ppermute | solution.py:682
  1086.4 8.8 slice-start.2
  1086.4 8.8 slice-start.3
  1086.4 8.8 slice-start.4
  1095.2 4.8 copy-start.6
  1095.2 6.5 copy-start.1
Sparse Core Ops, SparseCore 0:
  26.9 43.0 all-gather.13
  134.6 84.6 all-gather.15
  375.2 222.0 all-gather.29
  598.9 40.0 all-gather.19
  640.7 49.2 all-gather.25
  691.6 39.8 all-gather.17
  733.3 170.2 all-gather.31
  905.1 9.3 all-gather.27
  956.2 26.0 all-gather.23
  1004.8 25.9 all-gather.21
